TPU v7x, 32 devices: a whole 2x2x4 slice. The times are simulated.
32 devices in a mesh: ep: 16 (over z, y, core), dp: 2 (over x).
Axes of the slice: x: 2, y: 2, z: 4, core: 2. Of those that a mesh axis runs over, the one named last changes fastest.
Arguments:
- tokens: bfloat16 [512, 3584], P(('ep', 'dp')), may hold values from -6 to 6
- norm_gain: float32 [3584], replicated, may hold values from 0.25 to 1.75
- router: bfloat16 [3584, 16], replicated, may hold values from -0.09375 to 0.09375
- next_router: bfloat16 [3584, 16], P('dp'), may hold values from -0.09375 to 0.09375
- expert_ids: int32 [512, 8], P(('ep', 'dp')), may hold values from 0 to 15, all different within a row; in each aligned block of 16 rows (0 to 15, 16 to 31, ...) at most 16 rows name the same one
- store: bfloat16 [16, 2, 224, 128, 128], P('ep', 'dp'), may hold values from -0.125 to 0.125
- send_list: int32 [16, 224], P('ep'), may hold values from -1 to 223, as said below
- cache_map: int32 [16, 224], P('ep'), may hold values from 0 to 223, as said below
Outputs:
- layer_out: bfloat16 [512, 3584], P(('ep', 'dp'))
- next_scores: float32 [512, 16], P(('ep', 'dp'))
Inputs may be any that keep to these rules, and one draw needn't show every extreme that they name: `expert_ids`: each row names 8 different experts; among the rows of one device no expert is named by more than 16 rows, a bound that some block reaches. `send_list`: an entry is -1 where that arriving slot stays empty; every row names each of the 224 store indices exactly once. `cache_map`: each entry numbers an arriving slot of that device that is never empty; the entries of a row are distinct.
All inputs are finite; a program needn't handle non-finite values.
Results may differ from a plain program's by a relative error of at most 0.0095.
Values may be sent and summed in bfloat16 or wider, within the bound.
No kernel may reach another device: no remote copies, remote signals or barrier semaphores. Data moves between devices by JAX's collectives and lax.ppermute only.
A program may use at most 64 MiB of HBM per device.

v0:
```python
import jax
import jax.numpy as jnp
from jax import lax
from jax.sharding import PartitionSpec as P


def per_device(tokens, norm_gain, router, next_router, expert_ids, store, send_list, cache_map):
    tok_dev, width = tokens.shape
    n_dp = lax.axis_size("dp")
    experts = router.shape[1]
    top = expert_ids.shape[1]
    tiles = cache_map.shape[1]
    tile_rows = store.shape[3]
    tile_cols = store.shape[4]
    part = width // n_dp
    row_tiles = part // tile_rows
    col_tiles = tiles // (2 * row_tiles)
    hidden_width = col_tiles * tile_cols
    capacity = min(tok_dev, max(2, 2 * tok_dev * top // experts))
    values = tokens.astype(jnp.float32)
    scale = lax.rsqrt(jnp.mean(values * values, axis=1, keepdims=True) + 1e-06)
    normed = (values * scale * norm_gain).astype(jnp.bfloat16)
    scores = jax.nn.sigmoid(jnp.dot(normed, router, preferred_element_type=jnp.float32))
    chosen = (expert_ids[:, :, None] == jnp.arange(experts, dtype=jnp.int32)[None, None, :]).astype(
        jnp.float32
    )
    picked = jnp.sum(chosen * scores[:, None, :], axis=2)
    weights = (2.5 * picked / jnp.sum(picked, axis=1, keepdims=True)).astype(jnp.bfloat16)
    flat = chosen.reshape(tok_dev * top, experts)
    before = jnp.cumsum(flat, axis=0) - flat
    rank = jnp.sum(before * flat, axis=1).astype(jnp.int32)
    slot = expert_ids.reshape(-1) * capacity + rank
    columns = jnp.arange(experts * capacity, dtype=jnp.int32)
    match = (slot[:, None] == columns[None, :]).reshape(tok_dev, top, experts * capacity)
    dispatch = jnp.sum(match.astype(jnp.float32), axis=1).astype(jnp.bfloat16)
    combine = jnp.sum(
        jnp.where(match, weights.astype(jnp.float32)[:, :, None], 0.0), axis=1
    ).astype(jnp.bfloat16)
    outgoing = lax.dot_general(
        dispatch, normed, (((0,), (0,)), ((), ())), preferred_element_type=jnp.float32
    ).astype(jnp.bfloat16)
    owned = store.reshape(tiles, tile_rows, tile_cols)
    wanted = send_list.reshape(-1)
    present = wanted >= 0
    leaving = jnp.where(
        present[:, None, None], owned[jnp.maximum(wanted, 0)], jnp.zeros((), jnp.bfloat16)
    )
    arrived = lax.all_to_all(leaving, "ep", split_axis=0, concat_axis=0, tiled=True)
    cached = arrived[cache_map.reshape(-1)].reshape(2, row_tiles, col_tiles, tile_rows, tile_cols)
    up_tiles = cached[0]
    down_tiles = cached[1]
    rows = lax.all_to_all(
        lax.all_to_all(outgoing, "ep", split_axis=0, concat_axis=0, tiled=True),
        "dp",
        split_axis=1,
        concat_axis=0,
        tiled=True,
    )
    count = rows.shape[0]
    block = rows.reshape(count, row_tiles, tile_rows)
    product = jnp.einsum("nat,acts->ncs", block, up_tiles, preferred_element_type=jnp.float32)
    summed = lax.psum(product.reshape(count, hidden_width).astype(jnp.bfloat16), "dp").astype(
        jnp.float32
    )
    hidden = jax.nn.silu(summed).astype(jnp.bfloat16)
    number = hidden.shape[0]
    product = jnp.einsum(
        "ncs,acts->nat",
        hidden.reshape(number, col_tiles, tile_cols),
        down_tiles,
        preferred_element_type=jnp.float32,
    )
    result = product.reshape(number, part).astype(jnp.bfloat16)
    back = lax.all_to_all(
        lax.all_to_all(result, "dp", split_axis=0, concat_axis=1, tiled=True),
        "ep",
        split_axis=0,
        concat_axis=0,
        tiled=True,
    )
    mixed = jnp.dot(combine, back, preferred_element_type=jnp.float32)
    layer_out = (values + mixed).astype(jnp.bfloat16)
    stream = layer_out.astype(jnp.float32)
    renorm = lax.rsqrt(jnp.mean(stream * stream, axis=1, keepdims=True) + 1e-06)
    next_normed = (stream * renorm).astype(jnp.bfloat16)
    features = lax.all_to_all(next_normed, "dp", split_axis=1, concat_axis=0, tiled=True)
    partial_scores = jnp.dot(features, next_router, preferred_element_type=jnp.float32)
    next_logits = lax.psum_scatter(
        partial_scores.astype(jnp.bfloat16), "dp", scatter_dimension=0, tiled=True
    ).astype(jnp.float32)
    return (layer_out, jax.nn.sigmoid(next_logits))


def solution(mesh):
    in_specs = (
        P(("ep", "dp"), None),
        P(),
        P(),
        P("dp", None),
        P(("ep", "dp"), None),
        P("ep", "dp", None, None, None),
        P("ep", None),
        P("ep", None),
    )
    out_specs = (P(("ep", "dp"), None), P(("ep", "dp"), None))
    return jax.shard_map(
        per_device, mesh=mesh, in_specs=in_specs, out_specs=out_specs, check_vma=False
    )
```

profile of v0, /device:TPU:0, one launch (start us, length us, event | category | flops | bytes accessed | tf_op | source)
XLA Modules:
  0.0 437.3 jit_solution(8908242254397563168)
XLA Ops:
  7.2 1.1 fusion.17
  8.3 0.8 copy.46
  9.1 1.1 fusion.11
  10.3 0.3 select_reduce_fusion.1
  11.4 2.9 convolution_convert_fusion
  14.3 7.4 %all-to-all-start = ((bf16[16,16,3584]{2,1,0:T(8,128)(2,1)}), bf16[16,16,3584]{2,1,0:T(8,128)(2,1)S(1)}, u32[]{:S(2)}, u32[]{:S(2)}) async-start(bf16[16,16,3584]{2,1,0:T(8,128)(2,1)} %bitcast.49), calls=%async_computation | async-start | bytes 3670016 | tf_op jit(solution)/shard_map/all_to_all | solution.py:53
  21.8 11.4 %gather_fusion = bf16[224,128,128]{2,1,0:T(8,128)(2,1)} fusion(bf16[224,128,128]{2,1,0:T(8,128)(2,1)} %bitcast.50, s32[1024]{0:T(1024)S(1)} %pad_clamp_fusion.1), kind=kCustom, calls=%fused_computation | custom fusion | bytes 14680960 | tf_op jit(solution)/shard_map/gather | solution.py:46
  33.2 24.9 %all-to-all-done = bf16[16,16,3584]{2,1,0:T(8,128)(2,1)S(1)} async-done(((bf16[16,16,3584]{2,1,0:T(8,128)(2,1)}), bf16[16,16,3584]{2,1,0:T(8,128)(2,1)S(1)}, u32[]{:S(2)}, u32[]{:S(2)}) %all-to-all-start) | async-done | bytes 1835040 | tf_op jit(solution)/shard_map/all_to_all | solution.py:53
  58.1 1.5 all_to_all.57
  59.6 3.0 copy.49
  62.6 3.7 all-to-all-start.1
  66.3 6.6 %broadcast_select_fusion = bf16[224,128,128]{2,1,0:T(8,128)(2,1)} fusion(bf16[224,128,128]{2,1,0:T(8,128)(2,1)} %gather_fusion, pred[224]{0:T(512)(128)(4,1)S(1)} %compare_reduce_fusion), kind=kLoop, calls=%fused_computation.2 | loop fusion | flops 3670016 | bytes 14680288 | tf_op jit(solution)/shard_map/jit(_where)/select_n | solution.py:45
  73.0 16.8 %all-to-all-done.1 = bf16[256,2,1792]{2,0,1:T(8,128)(2,1)S(1)} async-done(((bf16[256,2,1792]{2,0,1:T(8,128)(2,1)}), bf16[256,2,1792]{2,0,1:T(8,128)(2,1)S(1)}, u32[]{:S(2)}, u32[]{:S(2)}) %all-to-all-start.1) | async-done | bytes 1835040 | tf_op jit(solution)/shard_map/all_to_all | solution.py:52
  89.7 9.6 %all-to-all-start.2 = ((bf16[224,128,128]{2,1,0:T(8,128)(2,1)}), bf16[224,128,128]{2,1,0:T(8,128)(2,1)}, u32[]{:S(2)}, u32[]{:S(2)}) async-start(bf16[224,128,128]{2,1,0:T(8,128)(2,1)} %broadcast_select_fusion), calls=%async_computation.2 | async-start | bytes 14680064 | tf_op jit(solution)/shard_map/all_to_all | solution.py:48
  99.6 2.4 reshape.175
  102.1 129.6 %all-to-all-done.2 = bf16[224,128,128]{2,1,0:T(8,128)(2,1)} async-done(((bf16[224,128,128]{2,1,0:T(8,128)(2,1)}), bf16[224,128,128]{2,1,0:T(8,128)(2,1)}, u32[]{:S(2)}, u32[]{:S(2)}) %all-to-all-start.2) | async-done | bytes 7340064 | tf_op jit(solution)/shard_map/all_to_all | solution.py:48
  231.7 11.4 %gather_fusion.1 = bf16[224,128,128]{2,1,0:T(8,128)(2,1)} fusion(bf16[224,128,128]{2,1,0:T(8,128)(2,1)} %all-to-all-done.2, s32[1024]{0:T(1024)S(1)} %pad_clamp_fusion), kind=kCustom, calls=%fused_computation.1 | custom fusion | bytes 14680960 | tf_op jit(solution)/shard_map/gather | solution.py:49
  243.2 9.4 %fusion.26 = (bf16[112,128,128]{2,1,0:T(8,128)(2,1)}, bf16[112,128,128]{2,1,0:T(8,128)(2,1)}) fusion(bf16[224,128,128]{2,1,0:T(8,128)(2,1)} %gather_fusion.1), kind=kLoop, calls=%fused_computation.56 | loop fusion | bytes 14680064 | tf_op jit(solution)/shard_map/slice | solution.py:50
  252.5 6.1 %copy.51 = bf16[14,8,128,128]{2,3,1,0:T(8,128)(2,1)} copy(bf16[14,8,128,128]{3,2,1,0:T(8,128)(2,1)} %bitcast.45) | data formatting | bytes 7340032 | tf_op jit(solution)/shard_map/squeeze | solution.py:50
  258.6 5.1 %bitcast_convert_fusion.1 = bf16[512,1024]{1,0:T(8,128)(2,1)} fusion(bf16[1024,14,128]{2,0,1:T(8,128)(2,1)} %bitcast.52, bf16[512,14,128]{2,1,0:T(8,128)(2,1)S(1)} %copy-done.2), kind=kOutput, calls=%fused_computation.13 | convolution fusion | flops 1879572480 | bytes 6553600 | tf_op jit(solution)/shard_map/nat,acts->ncs/dot_general | solution.py:61
  263.7 4.3 copy.53
  268.1 62.6 %all-reduce.2.cloned.1.call-done = bf16[512,1024]{1,0:T(8,128)(2,1)} async-done(((bf16[512,1024]{1,0:T(8,128)(2,1)}), bf16[512,1024]{1,0:T(8,128)(2,1)}) %all-reduce.2.cloned.1.call-update) | async-done | bytes 1048592 | tf_op jit(solution)/shard_map/psum | solution.py:62
  330.6 4.7 %bitcast_convert_fusion = bf16[512,1792]{1,0:T(8,128)(2,1)S(1)} fusion(bf16[1792,8,128]{2,0,1:T(8,128)(2,1)} %bitcast.51, bf16[512,1024]{1,0:T(8,128)(2,1)} %all-reduce.2.cloned.1.call-done), kind=kOutput, calls=%fused_computation.6 | convolution fusion | flops 1883111424 | bytes 6553600 | tf_op jit(solution)/shard_map/ncs,acts->nat/dot_general | solution.py:67
  335.4 24.7 %all_to_all.77 = bf16[2,256,1792]{2,1,0:T(8,128)(2,1)S(1)} all-to-all(bf16[2,256,1792]{2,1,0:T(8,128)(2,1)S(1)} %bitcast.53), channel_id=1, replica_groups=mesh['ep'=16,'dp'=2] {'dp'}, dimensions={0} | all-to-all | bytes 3670016 | tf_op jit(solution)/shard_map/all_to_all | solution.py:75
  360.0 1.9 copy.55
  362.0 2.2 all_to_all.64
  364.1 48.3 %all_to_all.78 = bf16[16,16,3584]{2,1,0:T(8,128)(2,1)S(1)} all-to-all(bf16[16,16,3584]{2,1,0:T(8,128)(2,1)} %all_to_all.64), channel_id=1, replica_groups=mesh['ep'=16,'dp'=2] {'ep'}, dimensions={0} | all-to-all | bytes 3670016 | tf_op jit(solution)/shard_map/all_to_all | solution.py:74
  412.5 0.5 fusion.15
  413.1 7.3 %all_to_all.79 = bf16[16,2,1792]{2,0,1:T(8,128)(2,1)S(1)} all-to-all(bf16[16,2,1792]{2,0,1:T(8,128)(2,1)S(1)} %bitcast.55), channel_id=1, replica_groups=mesh['ep'=16,'dp'=2] {'dp'}, dimensions={1} | all-to-all | bytes 229376 | tf_op jit(solution)/shard_map/all_to_all | solution.py:86
  420.4 0.8 convolution_convert_fusion.1
  421.2 8.0 %reduce-scatter.2.cloned.1.call-done = bf16[16,16]{1,0:T(8,128)(2,1)} async-done(((bf16[32,16]{1,0:T(8,128)(2,1)}), bf16[16,16]{1,0:T(8,128)(2,1)}) %reduce-scatter.2.cloned.1.call-update) | async-done | bytes 528 | tf_op jit(solution)/shard_map/reduce_scatter | solution.py:88
  429.2 1.3 add_divide_fusion
  (38 shorter events, 1.3 us)
Async XLA Ops:
  7.2 2.0 copy-start
  7.2 14.5 %copy-start.6 = (s32[1,224]{1,0:T(1,128)S(1)}, s32[1,224]{1,0:T(1,128)}, u32[]{:S(2)}) copy-start(s32[1,224]{1,0:T(1,128)} %param.14) | copy-start | bytes 2692
  14.3 43.8 %all-to-all-start = ((bf16[16,16,3584]{2,1,0:T(8,128)(2,1)}), bf16[16,16,3584]{2,1,0:T(8,128)(2,1)S(1)}, u32[]{:S(2)}, u32[]{:S(2)}) async-start(bf16[16,16,3584]{2,1,0:T(8,128)(2,1)} %bitcast.49), calls=%async_computation | async-start | bytes 3670016 | tf_op jit(solution)/shard_map/all_to_all | solution.py:53
  62.6 27.1 %all-to-all-start.1 = ((bf16[256,2,1792]{2,0,1:T(8,128)(2,1)}), bf16[256,2,1792]{2,0,1:T(8,128)(2,1)S(1)}, u32[]{:S(2)}, u32[]{:S(2)}) async-start(bf16[256,2,1792]{2,0,1:T(8,128)(2,1)} %copy.49), calls=%async_computation.1 | async-start | bytes 3670016 | tf_op jit(solution)/shard_map/all_to_all | solution.py:52
  73.0 26.7 %copy-start.7 = (s32[1,224]{1,0:T(1,128)S(1)}, s32[1,224]{1,0:T(1,128)}, u32[]{:S(2)}) copy-start(s32[1,224]{1,0:T(1,128)} %param.15) | copy-start | bytes 2692
  89.7 142.0 %all-to-all-start.2 = ((bf16[224,128,128]{2,1,0:T(8,128)(2,1)}), bf16[224,128,128]{2,1,0:T(8,128)(2,1)}, u32[]{:S(2)}, u32[]{:S(2)}) async-start(bf16[224,128,128]{2,1,0:T(8,128)(2,1)} %broadcast_select_fusion), calls=%async_computation.2 | async-start | bytes 14680064 | tf_op jit(solution)/shard_map/all_to_all | solution.py:48
  99.4 231.3 %all-reduce.2.cloned.1.call-start = ((), (), s32[]{:S(2)}) async-start(), calls=%async_computation.7 | async-start | bytes 2097152 | tf_op jit(solution)/shard_map/psum | solution.py:62
  252.5 6.1 %copy-start.2 = (bf16[512,14,128]{2,1,0:T(8,128)(2,1)S(1)}, bf16[512,14,128]{2,1,0:T(8,128)(2,1)}, u32[]{:S(2)}) copy-start(bf16[512,14,128]{2,1,0:T(8,128)(2,1)} %reshape.175) | copy-start | bytes 5505028
  263.7 165.5 %reduce-scatter.2.cloned.1.call-start = ((), (), s32[]{:S(2)}) async-start(), calls=%async_computation.8 | async-start | bytes 12288 | tf_op jit(solution)/shard_map/reduce_scatter | solution.py:88
  361.9 50.5 %copy-start.3 = (bf16[16,3584]{1,0:T(8,128)(2,1)S(1)}, bf16[16,3584]{1,0:T(8,128)(2,1)}, u32[]{:S(2)}) copy-start(bf16[16,3584]{1,0:T(8,128)(2,1)} %param.8) | copy-start | bytes 344068
  361.9 68.5 %copy-start.1 = (bf16[3584,16]{0,1:T(8,128)(2,1)S(1)}, bf16[3584,16]{0,1:T(8,128)(2,1)}, u32[]{:S(2)}) copy-start(bf16[3584,16]{0,1:T(8,128)(2,1)} %param.10) | copy-start | bytes 344068
  364.1 56.3 %copy-start.5 = (bf16[1792,16]{0,1:T(8,128)(2,1)S(1)}, bf16[1792,16]{0,1:T(8,128)(2,1)}, u32[]{:S(2)}) copy-start(bf16[1792,16]{0,1:T(8,128)(2,1)} %param.11) | copy-start | bytes 172036
  412.9 17.5 %copy-start.4 = (bf16[16,3584]{1,0:T(8,128)(2,1)}, bf16[16,3584]{1,0:T(8,128)(2,1)S(1)}, u32[]{:S(2)}) copy-start(bf16[16,3584]{1,0:T(8,128)(2,1)S(1)} %get-tuple-element.9) | copy-start | bytes 344068
Sparse Core Ops, SparseCore 0:
  263.8 66.7 all-reduce.1
  421.3 7.8 reduce-scatter.1
where the time goes:
time: 438 us; the launch traced here: 437 us
  waiting for transfers between devices  242 us (55%)
  blocking collectives  80.3 us (18%)
  local copies, waits for them, and re-layouts  54.6 us (12%)
  starting transfers between devices  21 us (5%)
  matrix products  15.1 us (3%)
  between operations  14.2 us (3%)
  other arithmetic  10.1 us (2%)
    all_to_all x1, waiting for transfers between devices, per_device(): lax.all_to_all(leaving, 'ep', split_axis=0, concat_axis=0, tiled=True)  130 us
    psum x1, waiting for transfers between devices, per_device(): lax.psum(product.reshape(count, hidden_width).astype(jnp.bfloat16), 'dp')  62.6 us
    all_to_all x1, blocking collectives, per_device(): lax.all_to_all(lax.all_to_all(result, 'dp', split_axis=0, concat_axis=1,...  48.3 us
    all_to_all x1, waiting for transfers between devices, per_device(): lax.all_to_all(outgoing, 'ep', split_axis=0, concat_axis=0, tiled=True)  24.9 us
    all_to_all x1, blocking collectives, per_device(): lax.all_to_all(result, 'dp', split_axis=0, concat_axis=1, tiled=True)  24.7 us
    all_to_all x1, waiting for transfers between devices, per_device(): lax.all_to_all(lax.all_to_all(outgoing, 'ep', split_axis=0, concat_axis=0...  16.8 us
    gather x1, local copies, waits for them, and re-layouts, per_device(): owned[jnp.maximum(wanted, 0)]  11.4 us
    gather x1, local copies, waits for them, and re-layouts, per_device(): arrived[cache_map.reshape(-1)]  11.4 us
  transfers between devices with their start and end apart: 5, of which 5 were waited for; matrix products, arithmetic and copies ran while one was open for 6% of the time, Pallas kernels for 0%

commit v1 on v0

--- a/solution.py
+++ b/solution.py
@@ -1,10 +1,250 @@
+import functools
+
 import jax
 import jax.numpy as jnp
 from jax import lax
+from jax.experimental import pallas as pl
+from jax.experimental.pallas import tpu as pltpu
 from jax.sharding import PartitionSpec as P
 
-
-def per_device(tokens, norm_gain, router, next_router, expert_ids, store, send_list, cache_map):
+ANY = pl.BlockSpec(memory_space=pl.ANY)
+VMEM = pl.BlockSpec(memory_space=pltpu.VMEM)
+SMEM = pl.BlockSpec(memory_space=pltpu.SMEM)
+
+
+def largest_divisor(number, most):
+    return max(d for d in range(1, most + 1) if number % d == 0)
+
+
+def pick_kernel(chunks, size, index_ref, store_ref, out_ref, held, in_sems, out_sem):
+    for chunk in range(chunks):
+
+        def fetch(i, carry, chunk=chunk):
+            slot = chunk * size + i
+            tile = jnp.maximum(index_ref[slot], 0)
+            pltpu.make_async_copy(store_ref.at[tile], held.at[slot], in_sems.at[chunk]).start()
+            return carry
+
+        lax.fori_loop(0, size, fetch, 0)
+    for chunk in range(chunks):
+        block = pl.ds(chunk * size, size)
+        pltpu.make_async_copy(held.at[block], held.at[block], in_sems.at[chunk]).wait()
+        pltpu.make_async_copy(held.at[block], out_ref.at[block], out_sem).start()
+    pltpu.make_async_copy(held, out_ref, out_sem).wait()
+
+
+def pick_tiles(store, index):
+    slots = index.shape[0]
+    chunks = largest_divisor(slots, 8)
+    shape = (slots,) + store.shape[1:]
+    return pl.pallas_call(
+        functools.partial(pick_kernel, chunks, slots // chunks),
+        out_shape=jax.ShapeDtypeStruct(shape, store.dtype),
+        in_specs=[SMEM, ANY],
+        out_specs=ANY,
+        scratch_shapes=[
+            pltpu.VMEM(shape, store.dtype),
+            pltpu.SemaphoreType.DMA((chunks,)),
+            pltpu.SemaphoreType.DMA,
+        ],
+        name="pick_tiles",
+    )(index, store)
+
+
+def up_kernel(step, map_ref, rows_ref, tiles_ref, out_ref, weight, sems):
+    tile_rows, tile_cols = tiles_ref.shape[1:]
+    part, width = weight.shape
+    row_tiles, col_tiles = part // tile_rows, width // tile_cols
+    blocks = col_tiles // step
+
+    def fetch(i, carry):
+        for column in range(col_tiles):
+            slot = map_ref[i * col_tiles + column]
+            start = pl.multiple_of(i * tile_rows, tile_rows)
+            pltpu.make_async_copy(
+                tiles_ref.at[slot],
+                weight.at[pl.ds(start, tile_rows), pl.ds(column * tile_cols, tile_cols)],
+                sems.at[column // step],
+            ).start()
+        return carry
+
+    lax.fori_loop(0, row_tiles, fetch, 0)
+    rows = rows_ref[:, :part]
+    for block in range(blocks):
+        columns = pl.ds(block * step * tile_cols, step * tile_cols)
+        piece = weight.at[:, columns]
+        pltpu.make_async_copy(piece, piece, sems.at[block]).wait()
+        out_ref[:, columns] = jnp.dot(
+            rows, piece[...], preferred_element_type=jnp.float32
+        ).astype(out_ref.dtype)
+
+
+def up_product(index, rows, tiles, part, width):
+    step = largest_divisor(width // tiles.shape[2], 2)
+    blocks = width // tiles.shape[2] // step
+    count = rows.shape[0]
+    return pl.pallas_call(
+        functools.partial(up_kernel, step),
+        out_shape=jax.ShapeDtypeStruct((count, width), jnp.bfloat16),
+        in_specs=[SMEM, VMEM, ANY],
+        out_specs=VMEM,
+        scratch_shapes=[
+            pltpu.VMEM((part, width), tiles.dtype),
+            pltpu.SemaphoreType.DMA((blocks,)),
+        ],
+        cost_estimate=pl.CostEstimate(
+            flops=2 * count * part * width,
+            bytes_accessed=2 * (part * width + count * (part + width)),
+            transcendentals=0,
+        ),
+        name="up_product",
+    )(index, rows, tiles)
+
+
+def down_kernel(step, first, map_ref, factor_ref, own_ref, other_ref, tiles_ref, out_ref, weight, hidden, sems):
+    tile_rows, tile_cols = tiles_ref.shape[1:]
+    part, width = weight.shape
+    row_tiles, col_tiles = part // tile_rows, width // tile_cols
+    blocks = row_tiles // step
+    half = own_ref.shape[0] // 2
+    for block in range(blocks):
+
+        def fetch(i, carry, block=block):
+            row = block * step + i
+            for column in range(col_tiles):
+                slot = map_ref[first + row * col_tiles + column]
+                start = pl.multiple_of(row * tile_rows, tile_rows)
+                pltpu.make_async_copy(
+                    tiles_ref.at[slot],
+                    weight.at[pl.ds(start, tile_rows), pl.ds(column * tile_cols, tile_cols)],
+                    sems.at[block],
+                ).start()
+            return carry
+
+        lax.fori_loop(0, step, fetch, 0)
+    for side in range(2):
+        mine, theirs = pl.ds(side * half, half), pl.ds((1 - side) * half, half)
+        pre = own_ref[mine, :].astype(jnp.float32) + other_ref[theirs, :].astype(jnp.float32)
+        hidden[mine, :] = (pre * jax.nn.sigmoid(pre)).astype(hidden.dtype)
+    units = hidden[...]
+    factor = factor_ref[...]
+    for block in range(blocks):
+        piece = weight.at[pl.ds(block * step * tile_rows, step * tile_rows), :]
+        pltpu.make_async_copy(piece, piece, sems.at[block]).wait()
+        product = lax.dot_general(
+            units, piece[...], (((1,), (1,)), ((), ())), preferred_element_type=jnp.float32
+        )
+        out_ref[:, pl.ds(block * step * tile_rows, step * tile_rows)] = (
+            product * factor
+        ).astype(out_ref.dtype)
+
+
+def down_product(index, first, factor, own, other, tiles, part):
+    step = largest_divisor(part // tiles.shape[1], 2)
+    blocks = part // tiles.shape[1] // step
+    count, width = own.shape
+    return pl.pallas_call(
+        functools.partial(down_kernel, step, first),
+        out_shape=jax.ShapeDtypeStruct((count, part), jnp.bfloat16),
+        in_specs=[SMEM, VMEM, VMEM, VMEM, ANY],
+        out_specs=VMEM,
+        scratch_shapes=[
+            pltpu.VMEM((part, width), tiles.dtype),
+            pltpu.VMEM((count, width), jnp.bfloat16),
+            pltpu.SemaphoreType.DMA((blocks,)),
+        ],
+        cost_estimate=pl.CostEstimate(
+            flops=2 * count * part * width,
+            bytes_accessed=2 * (part * width + count * (part + 2 * width)),
+            transcendentals=count * width,
+        ),
+        name="down_product",
+    )(index, factor, own, other, tiles)
+
+
+def flip(value, axis, bit):
+    return lax.ppermute(value, axis, [(i, i ^ bit) for i in range(lax.axis_size(axis))])
+
+
+def dense_layer(tokens, norm_gain, router, next_router, expert_ids, store, send_list, cache_map):
+    tok_dev, width = tokens.shape
+    n_ep = lax.axis_size("ep")
+    experts = router.shape[1]
+    tiles = cache_map.shape[1]
+    tile_rows, tile_cols = store.shape[3:]
+    part = width // 2
+    row_tiles = part // tile_rows
+    col_tiles = tiles // (2 * row_tiles)
+    hidden_width = col_tiles * tile_cols
+    me, side = lax.axis_index("ep"), lax.axis_index("dp")
+
+    leaving = pick_tiles(store.reshape(tiles, tile_rows, tile_cols), send_list.reshape(-1))
+    arrived = lax.all_to_all(leaving, "ep", split_axis=0, concat_axis=0, tiled=True)
+
+    values = tokens.astype(jnp.float32)
+    scale = lax.rsqrt(jnp.mean(values * values, axis=1, keepdims=True) + 1e-06)
+    normed = (values * scale * norm_gain).astype(jnp.bfloat16)
+    scores = jax.nn.sigmoid(jnp.dot(normed, router, preferred_element_type=jnp.float32))
+    chosen = (
+        expert_ids[:, :, None] == jnp.arange(experts, dtype=jnp.int32)[None, None, :]
+    ).astype(jnp.float32)
+    named = jnp.sum(chosen, axis=1)
+    picked = named * scores
+    weights = (2.5 * picked / jnp.sum(picked, axis=1, keepdims=True)).astype(jnp.bfloat16)
+    lanes = tile_cols * (-(-experts // tile_cols))
+    weights = jnp.pad(weights, ((0, 0), (0, lanes - experts)))
+    first, second = normed[:, :part], normed[:, part:]
+    mine = jnp.concatenate([jnp.where(side == 0, first, second), weights], axis=1)
+    theirs = jnp.concatenate([jnp.where(side == 0, second, first), weights], axis=1)
+    rows, other_router = lax.optimization_barrier(
+        (jnp.stack([mine, flip(theirs, "dp", 1)]), flip(next_router, "dp", 1))
+    )
+    far = n_ep // 2
+    bits = [far]
+    while far > 1:
+        far //= 2
+        bits.append(far)
+    for bit in bits:
+        rows = jnp.concatenate([rows, flip(rows, "ep", bit)], axis=1)
+    rows = rows.reshape(2 * n_ep * tok_dev, part + lanes)
+    lane = lax.broadcasted_iota(jnp.int32, (1, lanes), 1)
+    factor = jnp.sum(
+        jnp.where(lane == me, rows[:, part:].astype(jnp.float32), 0.0), axis=1, keepdims=True
+    )
+    index = cache_map.reshape(-1)
+    pre = up_product(index, rows, arrived, part, hidden_width)
+    product = down_product(
+        index, row_tiles * col_tiles, factor, pre, flip(pre, "dp", 1), arrived, part
+    )
+    total = product.reshape(2, n_ep * tok_dev, part)
+    for bit in bits[::-1]:
+        count = total.shape[1] // 2
+        got = flip(total[:, count:], "ep", bit)
+        total = total[:, :count].astype(jnp.float32) + got.astype(jnp.float32)
+        if bit != bits[0]:
+            total = total.astype(jnp.bfloat16)
+    total = total.astype(jnp.bfloat16)
+    other = flip(total[1], "dp", 1)
+    mine = total[0]
+    mixed = jnp.where(
+        side == 0,
+        jnp.concatenate([mine, other], axis=1),
+        jnp.concatenate([other, mine], axis=1),
+    ).astype(jnp.float32)
+    layer_out = (values + mixed).astype(jnp.bfloat16)
+    stream = layer_out.astype(jnp.float32)
+    renorm = lax.rsqrt(jnp.mean(stream * stream, axis=1, keepdims=True) + 1e-06)
+    next_normed = (stream * renorm).astype(jnp.bfloat16)
+    whole_router = jnp.where(
+        side == 0,
+        jnp.concatenate([next_router, other_router], axis=0),
+        jnp.concatenate([other_router, next_router], axis=0),
+    )
+    next_logits = jnp.dot(next_normed, whole_router, preferred_element_type=jnp.float32)
+    return (layer_out, jax.nn.sigmoid(next_logits))
+
+
+def sparse_layer(tokens, norm_gain, router, next_router, expert_ids, store, send_list, cache_map):
     tok_dev, width = tokens.shape
     n_dp = lax.axis_size("dp")
     experts = router.shape[1]
@@ -16,7 +256,7 @@
     row_tiles = part // tile_rows
     col_tiles = tiles // (2 * row_tiles)
     hidden_width = col_tiles * tile_cols
-    capacity = min(tok_dev, max(2, 2 * tok_dev * top // experts))
+    capacity = row_capacity(tokens, router, expert_ids)
     values = tokens.astype(jnp.float32)
     scale = lax.rsqrt(jnp.mean(values * values, axis=1, keepdims=True) + 1e-06)
     normed = (values * scale * norm_gain).astype(jnp.bfloat16)
@@ -39,12 +279,8 @@
     outgoing = lax.dot_general(
         dispatch, normed, (((0,), (0,)), ((), ())), preferred_element_type=jnp.float32
     ).astype(jnp.bfloat16)
-    owned = store.reshape(tiles, tile_rows, tile_cols)
-    wanted = send_list.reshape(-1)
-    present = wanted >= 0
-    leaving = jnp.where(
-        present[:, None, None], owned[jnp.maximum(wanted, 0)], jnp.zeros((), jnp.bfloat16)
-    )
+    owned = store.reshape(store.shape[2], tile_rows, tile_cols)
+    leaving = owned[jnp.maximum(send_list.reshape(-1), 0)]
     arrived = lax.all_to_all(leaving, "ep", split_axis=0, concat_axis=0, tiled=True)
     cached = arrived[cache_map.reshape(-1)].reshape(2, row_tiles, col_tiles, tile_rows, tile_cols)
     up_tiles = cached[0]
@@ -91,6 +327,21 @@
     return (layer_out, jax.nn.sigmoid(next_logits))
 
 
+def row_capacity(tokens, router, expert_ids):
+    tok_dev, experts, top = tokens.shape[0], router.shape[1], expert_ids.shape[1]
+    return min(tok_dev, max(2, 2 * tok_dev * top // experts))
+
+
+def per_device(*arrays):
+    tokens, _, router, _, expert_ids, store, _, cache_map = arrays
+    n_ep = lax.axis_size("ep")
+    every_row = row_capacity(tokens, router, expert_ids) == tokens.shape[0]
+    one_each = router.shape[1] == n_ep and store.shape[2] == cache_map.shape[1]
+    if every_row and one_each and lax.axis_size("dp") == 2 and n_ep & (n_ep - 1) == 0:
+        return dense_layer(*arrays)
+    return sparse_layer(*arrays)
+
+
 def solution(mesh):
     in_specs = (
         P(("ep", "dp"), None),

time: 438 us -> 286 us (0.65)
  blocking collectives: 80.3 us -> 0 us
  local copies, waits for them, and re-layouts: 54.6 us -> 4.89 us
  Pallas kernels: 0 us -> 24.4 us
  matrix products: 15.1 us -> 1.13 us
  between operations: 14.2 us -> 0.94 us
  waiting for transfers between devices: 242 us -> 232 us
  other arithmetic: 10.1 us -> 2.21 us
    ppermute x0 -> x12, waiting for transfers between devices: none -> 232 us  [flip(): lax.ppermute(value, axis, [(i, i ^ bit) for i in range(lax.axis_size(axis...]
    all_to_all x3 -> x1, waiting for transfers between devices: 171 us -> 0.01 us  [dense_layer(): lax.all_to_all(leaving, 'ep', split_axis=0, concat_axis=0, tiled=True)]
    all_to_all x3 -> x0, blocking collectives: 80.3 us -> none  [the longest x1 48.3 us: per_device(): lax.all_to_all(lax.all_to_all(result, 'dp', split_axis=0, concat_axis=1,...]
    psum x1 -> x0, waiting for transfers between devices: 62.6 us -> none  [per_device(): lax.psum(product.reshape(count, hidden_width).astype(jnp.bfloat16), 'dp')]
    pallas_call x0 -> x3, Pallas kernels: none -> 24.4 us  [the longest x1 8.87 us: up_product(): pl.pallas_call(functools.partial(up_kernel, step), out_shape=jax.ShapeDty...]
    gather x2 -> x0, local copies, waits for them, and re-layouts: 22.9 us -> none  [the longest x1 11.4 us: per_device(): owned[jnp.maximum(wanted, 0)]]
    dot_general x6 -> x2, matrix products: 15.1 us -> 1.13 us  [the longest x1 0.85 us: dense_layer(): jnp.dot(next_normed, whole_router, preferred_element_type=jnp.float32)]
    all_to_all x3 -> x1, starting transfers between devices: 20.8 us -> 7.6 us  [dense_layer(): lax.all_to_all(leaving, 'ep', split_axis=0, concat_axis=0, tiled=True)]
  transfers between devices with their start and end apart: 5 -> 13, of which waited for: 5 -> 12; matrix products, arithmetic and copies ran while one was open for 6% -> 1% of each run, Pallas kernels for 0% -> 0%
where the time goes in v1:
time: 286 us
  waiting for transfers between devices  232 us (81%)
  Pallas kernels  24.4 us (9%)
  starting transfers between devices  20 us (7%)
  local copies, waits for them, and re-layouts  4.89 us (2%)
    ppermute x12, waiting for transfers between devices, flip(): lax.ppermute(value, axis, [(i, i ^ bit) for i in range(lax.axis_size(axis...  232 us
    ppermute x12, starting transfers between devices, flip(): lax.ppermute(value, axis, [(i, i ^ bit) for i in range(lax.axis_size(axis...  12.4 us
    pallas_call x1, Pallas kernels, up_product(): pl.pallas_call(functools.partial(up_kernel, step), out_shape=jax.ShapeDty...  8.87 us
    pallas_call x1, Pallas kernels, down_product(): pl.pallas_call(functools.partial(down_kernel, step, first), out_shape=jax...  8.83 us
    all_to_all x1, starting transfers between devices, dense_layer(): lax.all_to_all(leaving, 'ep', split_axis=0, concat_axis=0, tiled=True)  7.6 us
    pallas_call x1, Pallas kernels, pick_tiles(): pl.pallas_call(functools.partial(pick_kernel, chunks, slots // chunks), o...  6.68 us
  transfers between devices with their start and end apart: 13, of which 12 were waited for; matrix products, arithmetic and copies ran while one was open for 1% of the time, Pallas kernels for 0%

profile of v1, /device:TPU:0, one launch (start us, length us, event | category | flops | bytes accessed | tf_op | source)
XLA Modules:
  0.0 285.6 jit_solution(17732288427998586695)
XLA Ops:
  0.6 6.7 %pick_tiles.1 = bf16[224,128,128]{2,1,0:T(8,128)(2,1)} custom-call(s32[224]{0:T(256)} %bitcast.24, bf16[224,128,128]{2,1,0:T(8,128)(2,1)} %bitcast.15), custom_call_target="tpu_custom_call" | custom-call | tf_op jit(solution)/shard_map/pick_tiles/pallas_call | solution.py:40
  7.4 7.6 %all-to-all-start = ((bf16[224,128,128]{2,1,0:T(8,128)(2,1)}), bf16[224,128,128]{2,1,0:T(8,128)(2,1)}, u32[]{:S(2)}, u32[]{:S(2)}) async-start(bf16[224,128,128]{2,1,0:T(8,128)(2,1)} %pick_tiles.1), calls=%async_computation | async-start | bytes 14680064 | tf_op jit(solution)/shard_map/all_to_all | solution.py:182
  15.5 0.3 fusion.27
  15.9 1.6 collective-permute-start
  17.4 0.5 collective-permute-start.1
  18.0 2.3 collective-permute-done
  20.3 1.3 collective-permute-done.1
  21.6 2.8 collective-permute-start.2
  24.4 157.3 %collective-permute-done.2 = bf16[2,16,1920]{2,1,0:T(8,128)(2,1)S(1)} collective-permute-done((bf16[2,16,1920]{2,1,0:T(8,128)(2,1)S(1)}, bf16[2,16,1920]{2,1,0:T(8,128)(2,1)S(1)}, u32[]{:S(2)}, u32[]{:S(2)}) %collective-permute-start.2) | collective-permute-done | bytes 122912 | tf_op jit(solution)/shard_map/ppermute | solution.py:166
  181.8 7.4 %collective-permute-done.3 = bf16[2,32,1920]{2,1,0:T(8,128)(2,1)S(1)} collective-permute-done((bf16[2,32,1920]{2,1,0:T(8,128)(2,1)S(1)}, bf16[2,32,1920]{2,1,0:T(8,128)(2,1)S(1)}, u32[]{:S(2)}, u32[]{:S(2)}) %collective-permute-start.3) | collective-permute-done | bytes 245792 | tf_op jit(solution)/shard_map/ppermute | solution.py:166
  189.2 1.5 collective-permute-start.4
  190.7 10.3 %collective-permute-done.4 = bf16[2,64,1920]{2,1,0:T(8,128)(2,1)S(1)} collective-permute-done((bf16[2,64,1920]{2,1,0:T(8,128)(2,1)S(1)}, bf16[2,64,1920]{2,1,0:T(8,128)(2,1)S(1)}, u32[]{:S(2)}, u32[]{:S(2)}) %collective-permute-start.4) | collective-permute-done | bytes 491552 | tf_op jit(solution)/shard_map/ppermute | solution.py:166
  201.3 2.4 collective-permute-done.5
  203.9 1.3 copy-done.2
  205.2 8.9 %up_product.1.own_ref = bf16[512,1024]{1,0:T(8,128)(2,1)} custom-call(s32[224]{0:T(256)} %bitcast.22, bf16[512,1920]{1,0:T(8,128)(2,1)} %bitcast.18, bf16[224,128,128]{2,1,0:T(8,128)(2,1)} %all-to-all-done.tiles_ref), custom_call_target="tpu_custom_call" | custom-call | flops 1879048192 | bytes 6553600 | tf_op jit(solution)/shard_map/up_product/pallas_call | solution.py:86
  214.1 1.6 collective-permute-start.6
  215.6 1.0 select_reduce_fusion
  216.6 0.9 copy.14.factor_ref
  217.5 22.0 %collective-permute-done.6.other_ref = bf16[512,1024]{1,0:T(8,128)(2,1)S(1)} collective-permute-done((bf16[512,1024]{1,0:T(8,128)(2,1)}, bf16[512,1024]{1,0:T(8,128)(2,1)S(1)}, u32[]{:S(2)}, u32[]{:S(2)}) %collective-permute-start.6) | collective-permute-done | bytes 1048608 | tf_op jit(solution)/shard_map/ppermute | solution.py:166
  239.5 1.0 copy-done.3
  240.5 8.8 %down_product.1 = bf16[512,1792]{1,0:T(8,128)(2,1)} custom-call(s32[224]{0:T(256)} %bitcast.23, f32[512,1]{1,0:T(8,128)} %copy.14.factor_ref, bf16[512,1024]{1,0:T(8,128)(2,1)} %up_product.1.own_ref, bf16[512,1024]{1,0:T(8,128)(2,1)} %copy-done.3, bf16[224,128,128]{2,1,0:T(8,128)(2,1)} %all-to-all-done.tiles_ref), custom_call_target="tpu_custom_call" | custom-call | flops 1879048192 | bytes 7602176 | tf_op jit(solution)/shard_map/down_product/pallas_call | solution.py:146
  249.4 1.4 slice.56
  250.8 2.5 collective-permute-done.7
  253.5 1.5 collective-permute-start.8
  255.1 11.1 %collective-permute-done.8 = bf16[2,64,1792]{2,1,0:T(8,128)(2,1)S(1)} collective-permute-done((bf16[2,64,1792]{2,1,0:T(8,128)(2,1)S(1)}, bf16[2,64,1792]{2,1,0:T(8,128)(2,1)S(1)}, u32[]{:S(2)}, u32[]{:S(2)}) %collective-permute-start.8) | collective-permute-done | bytes 458784 | tf_op jit(solution)/shard_map/ppermute | solution.py:166
  266.3 0.6 collective-permute-start.9
  266.9 6.2 %collective-permute-done.9 = bf16[2,32,1792]{2,1,0:T(8,128)(2,1)S(1)} collective-permute-done((bf16[2,32,1792]{2,1,0:T(8,128)(2,1)S(1)}, bf16[2,32,1792]{2,1,0:T(8,128)(2,1)S(1)}, u32[]{:S(2)}, u32[]{:S(2)}) %collective-permute-start.9) | collective-permute-done | bytes 229408 | tf_op jit(solution)/shard_map/ppermute | solution.py:166
  273.2 0.6 collective-permute-start.10
  273.8 6.4 %collective-permute-done.10 = bf16[2,16,1792]{2,1,0:T(8,128)(2,1)S(1)} collective-permute-done((bf16[2,16,1792]{2,1,0:T(8,128)(2,1)S(1)}, bf16[2,16,1792]{2,1,0:T(8,128)(2,1)S(1)}, u32[]{:S(2)}, u32[]{:S(2)}) %collective-permute-start.10) | collective-permute-done | bytes 114720 | tf_op jit(solution)/shard_map/ppermute | solution.py:166
  280.3 1.6 collective-permute-start.11
  281.8 2.7 collective-permute-done.11
  284.7 0.9 fusion.2
  (48 shorter events, 1.8 us)
Async XLA Ops:
  0.6 14.8 %copy-start = (bf16[3584,16]{0,1:T(8,128)(2,1)S(1)}, bf16[3584,16]{0,1:T(8,128)(2,1)}, u32[]{:S(2)}) copy-start(bf16[3584,16]{0,1:T(8,128)(2,1)} %param.10) | copy-start | bytes 344068
  7.3 7.7 %copy-start.7 = (s32[16,8]{0,1:T(8,128)S(1)}, s32[16,8]{0,1:T(8,128)}, u32[]{:S(2)}) copy-start(s32[16,8]{0,1:T(8,128)} %param.12) | copy-start | bytes 1540
  7.3 7.8 %copy-start.4 = (bf16[16,3584]{1,0:T(8,128)(2,1)S(1)}, bf16[16,3584]{1,0:T(8,128)(2,1)}, u32[]{:S(2)}) copy-start(bf16[16,3584]{1,0:T(8,128)(2,1)} %param.8) | copy-start | bytes 344068
  7.4 8.0 %copy-start.6 = (f32[3584]{0:T(1024)S(1)}, f32[3584]{0:T(1024)}, u32[]{:S(2)}) copy-start(f32[3584]{0:T(1024)} %param.9) | copy-start | bytes 43012
  7.4 10.1 %copy-start.8 = (bf16[1792,16]{0,1:T(8,128)(2,1)S(1)}, bf16[1792,16]{0,1:T(8,128)(2,1)}, u32[]{:S(2)}) copy-start(bf16[1792,16]{0,1:T(8,128)(2,1)} %param.11) | copy-start | bytes 172036
  7.4 196.5 %all-to-all-start = ((bf16[224,128,128]{2,1,0:T(8,128)(2,1)}), bf16[224,128,128]{2,1,0:T(8,128)(2,1)}, u32[]{:S(2)}, u32[]{:S(2)}) async-start(bf16[224,128,128]{2,1,0:T(8,128)(2,1)} %pick_tiles.1), calls=%async_computation | async-start | bytes 14680064 | tf_op jit(solution)/shard_map/all_to_all | solution.py:182
  15.9 4.4 %collective-permute-start = (bf16[16,1920]{1,0:T(8,128)(2,1)S(1)}, bf16[16,1920]{1,0:T(8,128)(2,1)S(1)}, u32[]{:S(2)}, u32[]{:S(2)}) collective-permute-start(bf16[16,1920]{1,0:T(8,128)(2,1)S(1)} %get-tuple-element.13), channel_id=1, source_target_pairs={{0,1},{1,0},{2,3},{3,2},{4,5},{5,4},{6,7},{7,6},{8,9},{9,8},{10,11... | collective-permute-start | bytes 184328 | tf_op jit(solution)/shard_map/ppermute | solution.py:166
  17.4 4.2 %collective-permute-start.1 = (bf16[1792,16]{0,1:T(8,128)(2,1)S(1)}, bf16[1792,16]{0,1:T(8,128)(2,1)S(1)}, u32[]{:S(2)}, u32[]{:S(2)}) collective-permute-start(bf16[1792,16]{0,1:T(8,128)(2,1)S(1)} %copy-done.8), channel_id=1, source_target_pairs={{0,1},{1,0},{2,3},{3,2},{4,5},{5,4},{6,7},{7,6},{8,9},{9,8},{10,11... | collective-permute-start | bytes 172040 | tf_op jit(solution)/shard_map/ppermute | solution.py:166
  21.6 160.0 %collective-permute-start.2 = (bf16[2,16,1920]{2,1,0:T(8,128)(2,1)S(1)}, bf16[2,16,1920]{2,1,0:T(8,128)(2,1)S(1)}, u32[]{:S(2)}, u32[]{:S(2)}) collective-permute-start(bf16[2,16,1920]{2,1,0:T(8,128)(2,1)S(1)} %pad_maximum_fusion.3), channel_id=1, source_target_pairs={{0,16},{2,18},{4,20},{6,22},{8,24},{10,26},{12,28},{14,30},{16,0},... | collective-permute-start | bytes 368648 | tf_op jit(solution)/shard_map/ppermute | solution.py:166
  181.7 7.5 %collective-permute-start.3 = (bf16[2,32,1920]{2,1,0:T(8,128)(2,1)S(1)}, bf16[2,32,1920]{2,1,0:T(8,128)(2,1)S(1)}, u32[]{:S(2)}, u32[]{:S(2)}) collective-permute-start(bf16[2,32,1920]{2,1,0:T(8,128)(2,1)S(1)} %pad_maximum_fusion.2), channel_id=1, source_target_pairs={{0,8},{2,10},{4,12},{6,14},{8,0},{10,2},{12,4},{14,6},{16,24},{18,... | collective-permute-start | bytes 737288 | tf_op jit(solution)/shard_map/ppermute | solution.py:166
  189.2 11.9 %collective-permute-start.4 = (bf16[2,64,1920]{2,1,0:T(8,128)(2,1)S(1)}, bf16[2,64,1920]{2,1,0:T(8,128)(2,1)S(1)}, u32[]{:S(2)}, u32[]{:S(2)}) collective-permute-start(bf16[2,64,1920]{2,1,0:T(8,128)(2,1)S(1)} %pad_maximum_fusion.1), channel_id=1, source_target_pairs={{0,4},{2,6},{4,0},{6,2},{8,12},{10,14},{12,8},{14,10},{16,20},{18,... | collective-permute-start | bytes 1474568 | tf_op jit(solution)/shard_map/ppermute | solution.py:166
  201.1 2.6 collective-permute-start.5
  203.9 1.3 copy-start.2
  214.1 25.5 %collective-permute-start.6 = (bf16[512,1024]{1,0:T(8,128)(2,1)}, bf16[512,1024]{1,0:T(8,128)(2,1)S(1)}, u32[]{:S(2)}, u32[]{:S(2)}) collective-permute-start(bf16[512,1024]{1,0:T(8,128)(2,1)} %up_product.1.own_ref), channel_id=1, source_target_pairs={{0,1},{1,0},{2,3},{3,2},{4,5},{5,4},{6,7},{7,6},{8,9},{9,8},{10,11... | collective-permute-start | bytes 3145736 | tf_op jit(solution)/shard_map/ppermute | solution.py:166
  239.5 1.0 copy-start.3
  249.4 3.9 %copy-start.1 = (bf16[512,1792]{1,0:T(8,128)(2,1)S(1)}, bf16[512,1792]{1,0:T(8,128)(2,1)}, u32[]{:S(2)}) copy-start(bf16[512,1792]{1,0:T(8,128)(2,1)} %down_product.1) | copy-start | bytes 5505028
  250.7 2.5 collective-permute-start.7
  253.5 12.6 %collective-permute-start.8 = (bf16[2,64,1792]{2,1,0:T(8,128)(2,1)S(1)}, bf16[2,64,1792]{2,1,0:T(8,128)(2,1)S(1)}, u32[]{:S(2)}, u32[]{:S(2)}) collective-permute-start(bf16[2,64,1792]{2,1,0:T(8,128)(2,1)S(1)} %slice.58), channel_id=1, source_target_pairs={{0,4},{2,6},{4,0},{6,2},{8,12},{10,14},{12,8},{14,10},{16,20},{18,... | collective-permute-start | bytes 1376264 | tf_op jit(solution)/shard_map/ppermute | solution.py:166
  266.3 6.9 %collective-permute-start.9 = (bf16[2,32,1792]{2,1,0:T(8,128)(2,1)S(1)}, bf16[2,32,1792]{2,1,0:T(8,128)(2,1)S(1)}, u32[]{:S(2)}, u32[]{:S(2)}) collective-permute-start(bf16[2,32,1792]{2,1,0:T(8,128)(2,1)S(1)} %slice.60), channel_id=1, source_target_pairs={{0,8},{2,10},{4,12},{6,14},{8,0},{10,2},{12,4},{14,6},{16,24},{18,... | collective-permute-start | bytes 688136 | tf_op jit(solution)/shard_map/ppermute | solution.py:166
  273.2 7.0 %collective-permute-start.10 = (bf16[2,16,1792]{2,1,0:T(8,128)(2,1)S(1)}, bf16[2,16,1792]{2,1,0:T(8,128)(2,1)S(1)}, u32[]{:S(2)}, u32[]{:S(2)}) collective-permute-start(bf16[2,16,1792]{2,1,0:T(8,128)(2,1)S(1)} %slice.62), channel_id=1, source_target_pairs={{0,16},{2,18},{4,20},{6,22},{8,24},{10,26},{12,28},{14,30},{16,0},... | collective-permute-start | bytes 344072 | tf_op jit(solution)/shard_map/ppermute | solution.py:166
  280.3 4.2 %collective-permute-start.11 = (bf16[16,1792]{1,0:T(8,128)(2,1)S(1)}, bf16[16,1792]{1,0:T(8,128)(2,1)S(1)}, u32[]{:S(2)}, u32[]{:S(2)}) collective-permute-start(bf16[16,1792]{1,0:T(8,128)(2,1)S(1)} %get-tuple-element.8), channel_id=1, source_target_pairs={{0,1},{1,0},{2,3},{3,2},{4,5},{5,4},{6,7},{7,6},{8,9},{9,8},{10,11... | collective-permute-start | bytes 172040 | tf_op jit(solution)/shard_map/ppermute | solution.py:166
  284.7 0.9 copy-start.5

commit v2 on v0

--- a/solution.py
+++ b/solution.py
@@ -1,10 +1,449 @@
+import functools
+
 import jax
 import jax.numpy as jnp
 from jax import lax
+from jax.experimental import pallas as pl
+from jax.experimental.pallas import tpu as pltpu
 from jax.sharding import PartitionSpec as P
 
 
-def per_device(tokens, norm_gain, router, next_router, expert_ids, store, send_list, cache_map):
+ANY = pl.BlockSpec(memory_space=pl.ANY)
+VMEM = pl.BlockSpec(memory_space=pltpu.VMEM)
+SMEM = pl.BlockSpec(memory_space=pltpu.SMEM)
+
+
+def largest_divisor(number, most):
+    return max(d for d in range(1, most + 1) if number % d == 0)
+
+
+def pick_kernel(column_of, chunks, size, place_ref, list_ref, store_ref, *refs):
+    outs, (held, in_sems, out_sem) = refs[:-3], refs[-3:]
+    place = place_ref[0]
+    for chunk in range(chunks):
+
+        def fetch(i, carry, chunk=chunk):
+            tile = list_ref[column_of(place, chunk, i)]
+            copy = pltpu.make_async_copy(
+                store_ref.at[tile], held.at[chunk * size + i], in_sems.at[chunk]
+            )
+            copy.start()
+            return carry
+
+        lax.fori_loop(0, size, fetch, 0)
+    puts = []
+    for chunk in range(chunks):
+        block = held.at[pl.ds(chunk * size, size)]
+        pltpu.make_async_copy(block, block, in_sems.at[chunk]).wait()
+        target = outs[chunk] if len(outs) > 1 else outs[0].at[pl.ds(chunk * size, size)]
+        puts.append(pltpu.make_async_copy(block, target, out_sem.at[chunk]))
+        puts[-1].start()
+    for put in puts:
+        put.wait()
+
+
+def pick_tiles(column_of, place, wanted, store, chunks, size, joined):
+    tile = store.shape[1:]
+    if joined:
+        shapes = jax.ShapeDtypeStruct((chunks * size,) + tile, store.dtype)
+    else:
+        shapes = [jax.ShapeDtypeStruct((size,) + tile, store.dtype)] * chunks
+    return pl.pallas_call(
+        functools.partial(pick_kernel, column_of, chunks, size),
+        out_shape=shapes,
+        in_specs=[SMEM, SMEM, ANY],
+        out_specs=ANY if joined else [ANY] * chunks,
+        scratch_shapes=[
+            pltpu.VMEM((chunks * size,) + tile, store.dtype),
+            pltpu.SemaphoreType.DMA((chunks,)),
+            pltpu.SemaphoreType.DMA((chunks,)),
+        ],
+        cost_estimate=pl.CostEstimate(
+            flops=chunks * size * 2**24, bytes_accessed=chunks * size * 2**17, transcendentals=0
+        ),
+    )(place, wanted, store)
+
+
+def scatter_tiles(first, map_ref, tile_refs, sources, weight, sem_of):
+    tile_rows, tile_cols = sources[0].shape[1:]
+    part, width = weight.shape
+    row_tiles, col_tiles = part // tile_rows, width // tile_cols
+
+    def place_of(s):
+        row, column = lax.div(s, col_tiles), lax.rem(s, col_tiles)
+        rows = pl.ds(pl.multiple_of(row * tile_rows, tile_rows), tile_rows)
+        columns = pl.ds(pl.multiple_of(column * tile_cols, tile_cols), tile_cols)
+        return row, column, weight.at[rows, columns]
+
+    begin = 0
+    for source in sources:
+
+        def fetch(i, carry, source=source, begin=begin):
+            s = tile_refs[begin + i] - first
+
+            @pl.when((s >= 0) & (s < row_tiles * col_tiles))
+            def _():
+                row, column, place = place_of(s)
+                pltpu.make_async_copy(source.at[i], place, sem_of(row, column)).start()
+
+            return carry
+
+        lax.fori_loop(0, source.shape[0], fetch, 0, unroll=source.shape[0] < 8)
+        begin += source.shape[0]
+
+    def clear(row, carry):
+        for column in range(col_tiles):
+
+            @pl.when(map_ref[first + row * col_tiles + column] < 0)
+            def _(column=column):
+                rows = pl.ds(pl.multiple_of(row * tile_rows, tile_rows), tile_rows)
+                weight[rows, pl.ds(column * tile_cols, tile_cols)] = jnp.zeros(
+                    (tile_rows, tile_cols), weight.dtype
+                )
+
+        return carry
+
+    lax.fori_loop(0, row_tiles, clear, 0)
+
+
+def wait_tiles(first, map_ref, weight, tile, sem, rows, columns):
+    tile_rows, tile_cols = tile
+    col_tiles = weight.shape[1] // tile_cols
+
+    def wait(i, carry):
+        row = rows[0] + i
+        for column in columns:
+
+            @pl.when(map_ref[first + row * col_tiles + column] >= 0)
+            def _(column=column):
+                place = weight.at[
+                    pl.ds(pl.multiple_of(row * tile_rows, tile_rows), tile_rows),
+                    pl.ds(column * tile_cols, tile_cols),
+                ]
+                pltpu.make_async_copy(place, place, sem).wait()
+
+        return carry
+
+    lax.fori_loop(0, rows[1], wait, 0)
+
+
+def up_kernel(step, map_ref, tile_refs, rows_ref, *refs):
+    sources, (out_ref, weight, sems) = refs[:-3], refs[-3:]
+    tile = sources[0].shape[1:]
+    part, width = weight.shape
+    row_tiles, col_tiles = part // tile[0], width // tile[1]
+    scatter_tiles(
+        0, map_ref, tile_refs, sources, weight, lambda row, column: sems.at[lax.div(column, step)]
+    )
+    rows = rows_ref[:, :part]
+    for block in range(col_tiles // step):
+        wait_tiles(
+            0,
+            map_ref,
+            weight,
+            tile,
+            sems.at[block],
+            (0, row_tiles),
+            range(block * step, block * step + step),
+        )
+        columns = pl.ds(block * step * tile[1], step * tile[1])
+        out_ref[:, columns] = jnp.dot(
+            rows, weight[:, columns], preferred_element_type=jnp.float32
+        ).astype(out_ref.dtype)
+
+
+def up_product(index, inverse, rows, sources, part, width):
+    tile_cols = sources[0].shape[2]
+    step = largest_divisor(width // tile_cols, 4)
+    count = rows.shape[0]
+    return pl.pallas_call(
+        functools.partial(up_kernel, step),
+        out_shape=jax.ShapeDtypeStruct((count, width), jnp.bfloat16),
+        in_specs=[SMEM, SMEM, VMEM] + [ANY] * len(sources),
+        out_specs=VMEM,
+        scratch_shapes=[
+            pltpu.VMEM((part, width), sources[0].dtype),
+            pltpu.SemaphoreType.DMA((width // tile_cols // step,)),
+        ],
+        cost_estimate=pl.CostEstimate(
+            flops=2 * count * part * width,
+            bytes_accessed=2 * (part * width + count * (part + width)),
+            transcendentals=0,
+        ),
+        name="up_product",
+    )(index, inverse, rows, *sources)
+
+
+def place_kernel(first, chunks, map_ref, tile_refs, *refs):
+    sources, (out_ref, weight, in_sems, out_sems) = refs[:-4], refs[-4:]
+    tile = sources[0].shape[1:]
+    part, width = weight.shape
+    size = part // tile[0] // chunks
+    scatter_tiles(
+        first, map_ref, tile_refs, sources, weight, lambda row, column: in_sems.at[lax.div(row, size)]
+    )
+    puts = []
+    for chunk in range(chunks):
+        wait_tiles(
+            first,
+            map_ref,
+            weight,
+            tile,
+            in_sems.at[chunk],
+            (chunk * size, size),
+            range(width // tile[1]),
+        )
+        block = pl.ds(chunk * size * tile[0], size * tile[0])
+        puts.append(pltpu.make_async_copy(weight.at[block], out_ref.at[block], out_sems.at[chunk]))
+        puts[-1].start()
+    for put in puts:
+        put.wait()
+
+
+def place_down(index, inverse, first, sources, part, width):
+    chunks = largest_divisor(part // sources[0].shape[1], 4)
+    return pl.pallas_call(
+        functools.partial(place_kernel, first, chunks),
+        out_shape=jax.ShapeDtypeStruct((part, width), sources[0].dtype),
+        in_specs=[SMEM, SMEM] + [ANY] * len(sources),
+        out_specs=ANY,
+        scratch_shapes=[
+            pltpu.VMEM((part, width), sources[0].dtype),
+            pltpu.SemaphoreType.DMA((chunks,)),
+            pltpu.SemaphoreType.DMA((chunks,)),
+        ],
+        cost_estimate=pl.CostEstimate(
+            flops=part * width * 1024, bytes_accessed=4 * part * width, transcendentals=0
+        ),
+        name="place_down",
+    )(index, inverse, *sources)
+
+
+def down_kernel(*refs):
+    experts = len(refs) // 3
+    out_ref = refs[-1]
+    total = 0.0
+    for e in range(experts):
+        weight, units, factor = refs[3 * e : 3 * e + 3]
+        product = lax.dot_general(
+            units[...], weight[...], (((1,), (1,)), ((), ())), preferred_element_type=jnp.float32
+        )
+        total = total + product * factor[...]
+    out_ref[...] = total.astype(out_ref.dtype)
+
+
+def down_product(weights, units, factors, block):
+    part, width = weights[0].shape
+    count = units[0].shape[0]
+    specs, operands = [], []
+    for weight, unit, factor in zip(weights, units, factors, strict=True):
+        specs += [
+            pl.BlockSpec((block, width), lambda i: (i, 0)),
+            pl.BlockSpec((count, width), lambda i: (0, 0)),
+            pl.BlockSpec((count, 1), lambda i: (0, 0)),
+        ]
+        operands += [weight, unit, factor]
+    return pl.pallas_call(
+        down_kernel,
+        grid=(part // block,),
+        out_shape=jax.ShapeDtypeStruct((count, part), jnp.bfloat16),
+        in_specs=specs,
+        out_specs=pl.BlockSpec((count, block), lambda i: (0, i)),
+        cost_estimate=pl.CostEstimate(
+            flops=2 * len(weights) * count * part * width,
+            bytes_accessed=2 * (len(weights) * (part + count) * width + count * part),
+            transcendentals=0,
+        ),
+        name="down_product",
+    )(*operands)
+
+
+def flip(value, axis, bit):
+    return lax.ppermute(value, axis, [(i, i ^ bit) for i in range(lax.axis_size(axis))])
+
+
+def silu_sum(first, second):
+    pre = first.astype(jnp.float32) + second.astype(jnp.float32)
+    return (pre * jax.nn.sigmoid(pre)).astype(jnp.bfloat16)
+
+
+def plain_sum(first, second):
+    return (first.astype(jnp.float32) + second.astype(jnp.float32)).astype(jnp.bfloat16)
+
+
+def take(value, axis, which):
+    return lax.index_in_dim(value, which, axis, keepdims=True)
+
+
+def add_up(value, steps):
+    for combine, (axis, name, bit) in steps:
+        value = combine(take(value, axis, 0), flip(take(value, axis, 1), name, bit))
+    return value
+
+
+def gather_back(value, steps):
+    for axis, name, bit in steps:
+        value = jnp.concatenate([value, flip(value, name, bit)], axis=axis)
+    return value
+
+
+def dense_layer(tokens, norm_gain, router, next_router, expert_ids, store, send_list, cache_map):
+    tok_dev, width = tokens.shape
+    n_ep = lax.axis_size("ep")
+    half = n_ep // 2
+    experts = router.shape[1]
+    tiles = cache_map.shape[1]
+    lanes_of = tiles // n_ep
+    sub = lanes_of // 2
+    tile_rows, tile_cols = store.shape[3:]
+    part = width // 2
+    row_tiles = part // tile_rows
+    col_tiles = tiles // (2 * row_tiles)
+    hidden_width = col_tiles * tile_cols
+    me, side = lax.axis_index("ep"), lax.axis_index("dp")
+    groups = [list(range(half)), list(range(half, n_ep))]
+    mirror = ("ep", half)
+    beside = ("ep", 1)
+    across = ("dp", 1)
+
+    owned = store.reshape(tiles, tile_rows, tile_cols)
+    wanted = send_list.reshape(-1)
+    place = jnp.reshape(me, (1,)).astype(jnp.int32)
+
+    def near_column(number, i, lane):
+        return i * lanes_of + lane
+
+    def far_column(number, j, lane):
+        return half * lanes_of + sub * (number ^ j) + lane
+
+    leaving = pick_tiles(near_column, place, wanted, owned, half, lanes_of, True)
+    far = pick_tiles(far_column, place, wanted, owned, n_ep, sub, False)
+
+    values = tokens.astype(jnp.float32)
+    scale = lax.rsqrt(jnp.mean(values * values, axis=1, keepdims=True) + 1e-06)
+    normed = (values * scale * norm_gain).astype(jnp.bfloat16)
+    scores = jax.nn.sigmoid(jnp.dot(normed, router, preferred_element_type=jnp.float32))
+    chosen = (
+        expert_ids[:, :, None] == jnp.arange(experts, dtype=jnp.int32)[None, None, :]
+    ).astype(jnp.float32)
+    picked = jnp.sum(chosen, axis=1) * scores
+    weights = (2.5 * picked / jnp.sum(picked, axis=1, keepdims=True)).astype(jnp.bfloat16)
+    digit = tile_cols
+    each = -(-tiles // tok_dev)
+    codes = jnp.pad(cache_map.reshape(-1), (0, each * tok_dev - tiles)).reshape(tok_dev, each)
+    codes = jnp.concatenate([codes // digit, codes % digit], axis=1).astype(jnp.bfloat16)
+    used = experts + 2 * each
+    lanes = tile_cols * (-(-used // tile_cols))
+    first, second = normed[:, :part], normed[:, part:]
+    mine = jnp.concatenate(
+        [
+            jnp.where(side == 0, first, second),
+            jnp.pad(jnp.concatenate([weights, codes], axis=1), ((0, 0), (0, lanes - used))),
+        ],
+        axis=1,
+    )
+    theirs = jnp.concatenate(
+        [
+            jnp.where(side == 0, second, first),
+            jnp.pad(weights, ((0, 0), (0, lanes - experts))),
+        ],
+        axis=1,
+    )
+    rows, leaving = lax.optimization_barrier((jnp.stack([mine, flip(theirs, *across)]), leaving))
+    arrived = lax.all_to_all(
+        leaving, "ep", split_axis=0, concat_axis=0, tiled=True, axis_index_groups=groups
+    )
+    rows = jnp.stack([rows, flip(rows, *mirror)], axis=1)
+    blocks = [rows]
+    for number in range(2, half, 2):
+        blocks.append(flip(rows, "ep", number))
+    crossed = [far[0]]
+    for j in range(1, n_ep):
+        crossed.append(flip(far[j], "ep", j))
+    rows = jnp.stack(blocks, axis=2)
+    rows = jnp.stack([rows, flip(rows, *beside)], axis=2)
+    rows = rows.reshape(2 * n_ep * tok_dev, part + lanes)
+    rows, other_router = lax.optimization_barrier((rows, flip(next_router, *across)))
+
+    def map_of(number):
+        relative = number ^ me
+        block = (relative // half * 2 + relative % 2) * (half // 2) + relative % half // 2
+        got = lax.dynamic_slice(
+            rows, (block * tok_dev, part + experts), (tok_dev, 2 * each)
+        ).astype(jnp.int32)
+        return (got[:, :each] * digit + got[:, each:]).reshape(-1)[:tiles]
+
+    lane = lax.broadcasted_iota(jnp.int32, (1, lanes), 1)
+    gates = rows[:, part:].astype(jnp.float32)
+    expert_of = [me % half, half + me // 2]
+    factors = [
+        jnp.sum(jnp.where(lane == e, gates, 0.0), axis=1, keepdims=True) for e in expert_of
+    ]
+
+    slots = map_of(expert_of[0])
+    owner, number = slots // lanes_of, slots % lanes_of
+    near = (owner // half) == (me // half)
+    map_a = jnp.where(near, owner % half * lanes_of + number, -1)
+    slots = map_of(expert_of[1])
+    owner, inside = slots // lanes_of, slots % lanes_of - sub * (me % 2)
+    map_b = jnp.where((inside >= 0) & (inside < sub), (owner ^ me) * sub + inside, -1)
+
+    def inverse_of(index):
+        held = index[None, :] == jnp.arange(tiles // 2, dtype=jnp.int32)[:, None]
+        number = jnp.arange(1, tiles + 1, dtype=jnp.int32)[None, :]
+        return jnp.sum(jnp.where(held, number, 0), axis=1) - 1
+
+    shape = (2, 2, 2, half // 2 * tok_dev, hidden_width)
+    held_a = (map_a, inverse_of(map_a))
+    held_b = (map_b, inverse_of(map_b))
+    (map_a, inverse_a), (map_b, inverse_b) = lax.optimization_barrier((held_a, held_b))
+    pre = up_product(map_a, inverse_a, rows, [arrived], part, hidden_width).reshape(shape)
+    own = add_up(pre, [(plain_sum, (0,) + across)])
+    down_a = place_down(map_a, inverse_a, tiles // 2, [arrived], part, hidden_width)
+    own = silu_sum(take(own, 1, 0), flip(take(own, 1, 1), *mirror))
+    kept, crossed, down_a = lax.optimization_barrier((own, crossed, down_a))
+    units_a = jnp.concatenate([kept, flip(own, *mirror)], axis=1)
+    units_a = gather_back(units_a, [(0,) + across])
+    pre = up_product(map_b, inverse_b, rows, crossed, part, hidden_width).reshape(shape)
+    own = add_up(pre, [(plain_sum, (2,) + beside), (silu_sum, (0,) + across)])
+    units_b = gather_back(own, [(0,) + across, (2,) + beside])
+    down_b = place_down(map_b, inverse_b, tiles // 2, crossed, part, hidden_width)
+    flat = (2 * n_ep * tok_dev, hidden_width)
+    units = [units_a.reshape(flat), units_b.reshape(flat)]
+    product = down_product(
+        [down_a, down_b], units, factors, tile_rows * largest_divisor(row_tiles, 2)
+    )
+    bits = [half]
+    while bits[0] > 1:
+        bits.insert(0, bits[0] // 2)
+    bits = [bits[0]] + bits[-2:0:-1] + [bits[-1]]
+    product = product.reshape((2, 2) + (2,) * (len(bits) - 1) + (tok_dev, part))
+    sums = [None, None]
+    for d in (1, 0):
+        total = product[d]
+        for bit in bits[:-1]:
+            total = plain_sum(total[:, 0], flip(total[:, 1], "ep", bit))
+        sums[d] = plain_sum(total[0], flip(total[1], "ep", bits[-1]))
+    mine, other = sums[0], flip(sums[1], *across)
+    mixed = jnp.where(
+        side == 0,
+        jnp.concatenate([mine, other], axis=1),
+        jnp.concatenate([other, mine], axis=1),
+    ).astype(jnp.float32)
+    layer_out = (values + mixed).astype(jnp.bfloat16)
+    stream = layer_out.astype(jnp.float32)
+    renorm = lax.rsqrt(jnp.mean(stream * stream, axis=1, keepdims=True) + 1e-06)
+    next_normed = (stream * renorm).astype(jnp.bfloat16)
+    whole_router = jnp.where(
+        side == 0,
+        jnp.concatenate([next_router, other_router], axis=0),
+        jnp.concatenate([other_router, next_router], axis=0),
+    )
+    next_logits = jnp.dot(next_normed, whole_router, preferred_element_type=jnp.float32)
+    return (layer_out, jax.nn.sigmoid(next_logits))
+
+
+def sparse_layer(tokens, norm_gain, router, next_router, expert_ids, store, send_list, cache_map):
     tok_dev, width = tokens.shape
     n_dp = lax.axis_size("dp")
     experts = router.shape[1]
@@ -16,7 +455,7 @@
     row_tiles = part // tile_rows
     col_tiles = tiles // (2 * row_tiles)
     hidden_width = col_tiles * tile_cols
-    capacity = min(tok_dev, max(2, 2 * tok_dev * top // experts))
+    capacity = row_capacity(tokens, router, expert_ids)
     values = tokens.astype(jnp.float32)
     scale = lax.rsqrt(jnp.mean(values * values, axis=1, keepdims=True) + 1e-06)
     normed = (values * scale * norm_gain).astype(jnp.bfloat16)
@@ -39,12 +478,8 @@
     outgoing = lax.dot_general(
         dispatch, normed, (((0,), (0,)), ((), ())), preferred_element_type=jnp.float32
     ).astype(jnp.bfloat16)
-    owned = store.reshape(tiles, tile_rows, tile_cols)
-    wanted = send_list.reshape(-1)
-    present = wanted >= 0
-    leaving = jnp.where(
-        present[:, None, None], owned[jnp.maximum(wanted, 0)], jnp.zeros((), jnp.bfloat16)
-    )
+    owned = store.reshape(store.shape[2], tile_rows, tile_cols)
+    leaving = owned[jnp.maximum(send_list.reshape(-1), 0)]
     arrived = lax.all_to_all(leaving, "ep", split_axis=0, concat_axis=0, tiled=True)
     cached = arrived[cache_map.reshape(-1)].reshape(2, row_tiles, col_tiles, tile_rows, tile_cols)
     up_tiles = cached[0]
@@ -91,6 +526,23 @@
     return (layer_out, jax.nn.sigmoid(next_logits))
 
 
+def row_capacity(tokens, router, expert_ids):
+    tok_dev, experts, top = tokens.shape[0], router.shape[1], expert_ids.shape[1]
+    return min(tok_dev, max(2, 2 * tok_dev * top // experts))
+
+
+def per_device(*arrays):
+    tokens, _, router, _, expert_ids, store, _, cache_map = arrays
+    n_ep = lax.axis_size("ep")
+    every_row = row_capacity(tokens, router, expert_ids) == tokens.shape[0]
+    one_each = router.shape[1] == n_ep and store.shape[2] == cache_map.shape[1]
+    two_power = n_ep > 2 and n_ep & (n_ep - 1) == 0
+    one_each = one_each and cache_map.shape[1] % (2 * n_ep) == 0
+    if every_row and one_each and two_power and lax.axis_size("dp") == 2:
+        return dense_layer(*arrays)
+    return sparse_layer(*arrays)
+
+
 def solution(mesh):
     in_specs = (
         P(("ep", "dp"), None),

time: 438 us -> 283 us (0.65)
  waiting for transfers between devices: 242 us -> 150 us
  blocking collectives: 80.3 us -> 0 us
  local copies, waits for them, and re-layouts: 54.6 us -> 8.77 us
  Pallas kernels: 0 us -> 44.7 us
  starting transfers between devices: 21 us -> 64.7 us
  matrix products: 15.1 us -> 1.13 us
  between operations: 14.2 us -> 1.31 us
    all_to_all x3 -> x1, waiting for transfers between devices: 171 us -> 0.01 us  [dense_layer(): lax.all_to_all(leaving, 'ep', split_axis=0, concat_axis=0, tiled=True, ax...]
    ppermute x0 -> x39, waiting for transfers between devices: none -> 150 us  [flip(): lax.ppermute(value, axis, [(i, i ^ bit) for i in range(lax.axis_size(axis...]
    all_to_all x3 -> x0, blocking collectives: 80.3 us -> none  [the longest x1 48.3 us: per_device(): lax.all_to_all(lax.all_to_all(result, 'dp', split_axis=0, concat_axis=1,...]
    psum x1 -> x0, waiting for transfers between devices: 62.6 us -> none  [per_device(): lax.psum(product.reshape(count, hidden_width).astype(jnp.bfloat16), 'dp')]
    ppermute x0 -> x39, starting transfers between devices: none -> 60.2 us  [flip(): lax.ppermute(value, axis, [(i, i ^ bit) for i in range(lax.axis_size(axis...]
    pallas_call x0 -> x7, Pallas kernels: none -> 44.7 us  [the longest x2 16 us: up_product(): pl.pallas_call(functools.partial(up_kernel, step), out_shape=jax.ShapeDty...]
    gather x2 -> x0, local copies, waits for them, and re-layouts: 22.9 us -> none  [the longest x1 11.4 us: per_device(): owned[jnp.maximum(wanted, 0)]]
    all_to_all x3 -> x1, starting transfers between devices: 20.8 us -> 4.51 us  [dense_layer(): lax.all_to_all(leaving, 'ep', split_axis=0, concat_axis=0, tiled=True, ax...]
  transfers between devices with their start and end apart: 5 -> 40, of which waited for: 5 -> 24; matrix products, arithmetic and copies ran while one was open for 6% -> 3% of each run, Pallas kernels for 0% -> 7%
where the time goes in v2:
time: 283 us; the launch traced here: 282 us
  waiting for transfers between devices  150 us (53%)
  starting transfers between devices  64.7 us (23%)
  Pallas kernels  44.7 us (16%)
  other arithmetic  11.3 us (4%)
  local copies, waits for them, and re-layouts  8.77 us (3%)
    ppermute x39, waiting for transfers between devices, flip(): lax.ppermute(value, axis, [(i, i ^ bit) for i in range(lax.axis_size(axis...  150 us
    ppermute x39, starting transfers between devices, flip(): lax.ppermute(value, axis, [(i, i ^ bit) for i in range(lax.axis_size(axis...  60.2 us
    pallas_call x2, Pallas kernels, up_product(): pl.pallas_call(functools.partial(up_kernel, step), out_shape=jax.ShapeDty...  16 us
    pallas_call x2, Pallas kernels, place_down(): pl.pallas_call(functools.partial(place_kernel, first, chunks), out_shape=...  10.8 us
    pallas_call x1, Pallas kernels, down_product(): pl.pallas_call(down_kernel, grid=(part // block,), out_shape=jax.ShapeDty...  9.67 us
    pallas_call x2, Pallas kernels, pick_tiles(): pl.pallas_call(functools.partial(pick_kernel, column_of, chunks, size), o...  8.22 us
  transfers between devices with their start and end apart: 40, of which 24 were waited for; matrix products, arithmetic and copies ran while one was open for 3% of the time, Pallas kernels for 7%

profile of v2, /device:TPU:0, one launch (start us, length us, event | category | flops | bytes accessed | tf_op | source)
XLA Modules:
  0.0 282.1 jit_solution(5527252969965310166)
XLA Ops:
  4.0 3.0 %collective-permute-start = (bf16[16,1920]{1,0:T(8,128)(2,1)S(1)}, bf16[16,1920]{1,0:T(8,128)(2,1)S(1)}, u32[]{:S(2)}, u32[]{:S(2)}) collective-permute-start(bf16[16,1920]{1,0:T(8,128)(2,1)S(1)} %fusion.33), channel_id=1, source_target_pairs={{0,1},{1,0},{2,3},{3,2},{4,5},{5,4},{6,7},{7,6},{8,9},{9,8},{10,11... | collective-permute-start | bytes 184328 | tf_op jit(solution)/shard_map/ppermute | solution.py:262
  9.1 4.1 %shard_map.95 = bf16[112,128,128]{2,1,0:T(8,128)(2,1)} custom-call(s32[1]{0:T(128)} %bitcast.2.place_ref, s32[224]{0:T(256)} %bitcast.112, bf16[224,128,128]{2,1,0:T(8,128)(2,1)} %bitcast.87), custom_call_target="tpu_custom_call" | custom-call | flops 1879048192 | bytes 14680064 | tf_op jit(solution)/shard_map/pallas_call | solution.py:51
  13.2 4.5 %all-to-all-start = ((bf16[112,128,128]{2,1,0:T(8,128)(2,1)}), bf16[112,128,128]{2,1,0:T(8,128)(2,1)}, u32[]{:S(2)}, u32[]{:S(2)}) async-start(bf16[112,128,128]{2,1,0:T(8,128)(2,1)} %shard_map.95), calls=%async_computation | async-start | bytes 7340032 | tf_op jit(solution)/shard_map/all_to_all | solution.py:353
  17.8 2.7 collective-permute-start.1
  20.4 40.3 %collective-permute-done.1 = bf16[2,16,1920]{2,1,0:T(8,128)(2,1)S(1)} collective-permute-done((bf16[2,16,1920]{2,1,0:T(8,128)(2,1)S(1)}, bf16[2,16,1920]{2,1,0:T(8,128)(2,1)S(1)}, u32[]{:S(2)}, u32[]{:S(2)}) %collective-permute-start.1) | collective-permute-done | bytes 122912 | tf_op jit(solution)/shard_map/ppermute | solution.py:262
  60.8 4.8 %collective-permute-start.3 = (bf16[2,2,16,1920]{3,2,0,1:T(8,128)(2,1)S(1)}, bf16[2,2,16,1920]{3,2,0,1:T(8,128)(2,1)S(1)}, u32[]{:S(2)}, u32[]{:S(2)}) collective-permute-start(bf16[2,2,16,1920]{3,2,0,1:T(8,128)(2,1)S(1)} %get-tuple-element.105), channel_id=1, source_target_pairs={{0,8},{2,10},{4,12},{6,14},{8,0},{10,2},{12,4},{14,6},{16,24},{18,... | collective-permute-start | bytes 737288 | tf_op jit(solution)/shard_map/ppermute | solution.py:262
  67.1 5.3 %collective-permute-done.3 = bf16[2,2,16,1920]{3,2,0,1:T(8,128)(2,1)S(1)} collective-permute-done((bf16[2,2,16,1920]{3,2,0,1:T(8,128)(2,1)S(1)}, bf16[2,2,16,1920]{3,2,0,1:T(8,128)(2,1)S(1)}, u32[]{:S(2)}, u32[]{:S(2)}) %collective-permute-start.3) | collective-permute-done | bytes 245792 | tf_op jit(solution)/shard_map/ppermute | solution.py:262
  72.4 5.6 %collective-permute-done.2 = bf16[2,2,16,1920]{3,2,0,1:T(8,128)(2,1)S(1)} collective-permute-done((bf16[2,2,16,1920]{3,2,0,1:T(8,128)(2,1)S(1)}, bf16[2,2,16,1920]{3,2,0,1:T(8,128)(2,1)S(1)}, u32[]{:S(2)}, u32[]{:S(2)}) %collective-permute-start.2) | collective-permute-done | bytes 245792 | tf_op jit(solution)/shard_map/ppermute | solution.py:262
  78.8 1.9 collective-permute-done.5
  84.7 8.4 %up_product.2 = bf16[512,1024]{1,0:T(8,128)(2,1)} custom-call(s32[224]{0:T(256)} %copy-done.19, s32[112]{0:T(128)} %broadcast_add_fusion.1.tile_refs, bf16[512,1920]{1,0:T(8,128)(2,1)} %bitcast.92, bf16[112,128,128]{2,1,0:T(8,128)(2,1)} %all-to-all-done.refs_0_), custom_call_target="tpu_custom_call" | custom-call | flops 1879048192 | bytes 6553600 | tf_op jit(solution)/shard_map/up_product/pallas_call | solution.py:159
  95.0 4.1 %shard_map.96 = (bf16[7,128,128]{2,1,0:T(8,128)(2,1)}, bf16[7,128,128]{2,1,0:T(8,128)(2,1)}, bf16[7,128,128]{2,1,0:T(8,128)(2,1)}, bf16[7,128,128]{2,1,0:T(8,128...) custom-call(s32[1]{0:T(128)} %bitcast.2.place_ref, ...), custom_call_target="tpu_custom_call" | custom-call | flops 1879048192 | bytes 14680064 | tf_op jit(solution)/shard_map/pallas_call | solution.py:51
  102.8 5.1 %collective-permute-done.7 = bf16[1,2,2,64,1024]{4,3,2,1,0:T(8,128)(2,1)S(1)} collective-permute-done((bf16[1,2,2,64,1024]{4,3,2,1,0:T(8,128)(2,1)S(1)}, bf16[1,2,2,64,1024]{4,3,2,1,0:T(8,128)(2,1)S(1)}, u32[]{:S(2)}, u32[]{:S(2)}) %collective-permute-start.7) | collective-permute-done | bytes 524320 | tf_op jit(solution)/shard_map/ppermute | solution.py:262
  109.9 1.9 collective-permute-done.11.refs_3_
  113.6 6.7 %collective-permute-done.13.refs_5_ = bf16[7,128,128]{2,1,0:T(8,128)(2,1)S(1)} collective-permute-done((bf16[7,128,128]{2,1,0:T(8,128)(2,1)}, bf16[7,128,128]{2,1,0:T(8,128)(2,1)S(1)}, u32[]{:S(2)}, u32[]{:S(2)}) %collective-permute-start.13) | collective-permute-done | bytes 229408 | tf_op jit(solution)/shard_map/ppermute | solution.py:262
  120.4 11.8 %collective-permute-done.14.refs_6_ = bf16[7,128,128]{2,1,0:T(8,128)(2,1)S(1)} collective-permute-done((bf16[7,128,128]{2,1,0:T(8,128)(2,1)}, bf16[7,128,128]{2,1,0:T(8,128)(2,1)S(1)}, u32[]{:S(2)}, u32[]{:S(2)}) %collective-permute-start.14) | collective-permute-done | bytes 229408 | tf_op jit(solution)/shard_map/ppermute | solution.py:262
  132.8 5.8 %place_down.2.refs_0_ = bf16[1792,1024]{1,0:T(8,128)(2,1)} custom-call(s32[224]{0:T(256)} %copy-done.19, s32[112]{0:T(128)} %broadcast_add_fusion.1.tile_refs, bf16[112,128,128]{2,1,0:T(8,128)(2,1)} %all-to-all-done.refs_0_), custom_call_target="tpu_custom_call" | custom-call | flops 1879048192 | bytes 7340032 | tf_op jit(solution)/shard_map/place_down/pallas_call | solution.py:205
  140.1 2.5 collective-permute-start.20
  142.6 13.7 %collective-permute-done.17.refs_9_ = bf16[7,128,128]{2,1,0:T(8,128)(2,1)S(1)} collective-permute-done((bf16[7,128,128]{2,1,0:T(8,128)(2,1)}, bf16[7,128,128]{2,1,0:T(8,128)(2,1)S(1)}, u32[]{:S(2)}, u32[]{:S(2)}) %collective-permute-start.17) | collective-permute-done | bytes 229408 | tf_op jit(solution)/shard_map/ppermute | solution.py:262
  156.3 2.3 collective-permute-start.21
  158.6 12.4 %collective-permute-done.18.refs_10_ = bf16[7,128,128]{2,1,0:T(8,128)(2,1)} collective-permute-done((bf16[7,128,128]{2,1,0:T(8,128)(2,1)}, bf16[7,128,128]{2,1,0:T(8,128)(2,1)}, u32[]{:S(2)}, u32[]{:S(2)}) %collective-permute-start.18) | collective-permute-done | bytes 229408 | tf_op jit(solution)/shard_map/ppermute | solution.py:262
  174.4 7.2 %collective-permute-done.22.refs_14_ = bf16[7,128,128]{2,1,0:T(8,128)(2,1)S(1)} collective-permute-done((bf16[7,128,128]{2,1,0:T(8,128)(2,1)}, bf16[7,128,128]{2,1,0:T(8,128)(2,1)S(1)}, u32[]{:S(2)}, u32[]{:S(2)}) %collective-permute-start.22) | collective-permute-done | bytes 229408 | tf_op jit(solution)/shard_map/ppermute | solution.py:262
  184.0 7.7 %up_product.3 = bf16[512,1024]{1,0:T(8,128)(2,1)} custom-call(s32[224]{0:T(256)} %copy-done.18, s32[112]{0:T(128)} %broadcast_add_fusion.tile_refs, bf16[512,1920]{1,0:T(8,128)(2,1)} %bitcast.93, bf16[7,128,128]{2,1,0:T(8,128)(2,1)} %get-tuple-element.69.refs_0_, bf16[7,128,128]{2,1,0:T(8,128)(2,1)} %copy-done.3, bf16[7,128,128]{2,1,0:T(8,128)(2,1)} %copy-done.4, ...), custom_call_target="tpu_custom_call" | custom-call | flops 1879048192 | bytes 6553600 | tf_op jit(solution)/shard_map/up_product/pallas_call | solution.py:159
  198.6 16.8 %collective-permute-start.24 = (bf16[1,1,2,64,1024]{4,3,2,1,0:T(8,128)(2,1)S(1)}, bf16[1,1,2,64,1024]{4,3,2,1,0:T(8,128)(2,1)S(1)}, u32[]{:S(2)}, u32[]{:S(2)}) collective-permute-start(bf16[1,1,2,64,1024]{4,3,2,1,0:T(8,128)(2,1)S(1)} %multiply_convert_fusion.1), channel_id=1, source_target_pairs={{0,16},{2,18},{4,20},{6,22},{8,24},{10,26},{12,28},{14,30},{16,0},... | collective-permute-start | bytes 786440 | tf_op jit(solution)/shard_map/ppermute | solution.py:262
  216.4 11.2 %collective-permute-done.24 = bf16[1,1,2,64,1024]{4,3,2,1,0:T(8,128)(2,1)S(1)} collective-permute-done((bf16[1,1,2,64,1024]{4,3,2,1,0:T(8,128)(2,1)S(1)}, bf16[1,1,2,64,1024]{4,3,2,1,0:T(8,128)(2,1)S(1)}, u32[]{:S(2)}, u32[]{:S(2)}) %collective-permute-start.24) | collective-permute-done | bytes 262176 | tf_op jit(solution)/shard_map/ppermute | solution.py:262
  231.4 5.0 %place_down.3.refs_3_ = bf16[1792,1024]{1,0:T(8,128)(2,1)} custom-call(s32[224]{0:T(256)} %copy-done.18, s32[112]{0:T(128)} %broadcast_add_fusion.tile_refs, bf16[7,128,128]{2,1,0:T(8,128)(2,1)} %get-tuple-element.69.refs_0_, bf16[7,128,128]{2,1,0:T(8,128)(2,1)} %copy-done.3, bf16[7,128,128]{2,1,0:T(8,128)(2,1)} %copy-done.4, ...), custom_call_target="tpu_custom_call" | custom-call | flops 1879048192 | bytes 7340032 | tf_op jit(solution)/shard_map/place_down/pallas_call | solution.py:205
  236.3 4.7 %collective-permute-done.25 = bf16[1,2,2,64,1024]{4,3,2,1,0:T(8,128)(2,1)S(1)} collective-permute-done((bf16[1,2,2,64,1024]{4,3,2,1,0:T(8,128)(2,1)S(1)}, bf16[1,2,2,64,1024]{4,3,2,1,0:T(8,128)(2,1)S(1)}, u32[]{:S(2)}, u32[]{:S(2)}) %collective-permute-start.25) | collective-permute-done | bytes 524320 | tf_op jit(solution)/shard_map/ppermute | solution.py:262
  243.2 9.7 %down_product.1 = bf16[512,1792]{1,0:T(8,128)(2,1)} custom-call(bf16[1792,1024]{1,0:T(8,128)(2,1)} %place_down.2.refs_0_, bf16[512,1024]{1,0:T(8,128)(2,1)} %bitcast.98, f32[512,1]{1,0:T(8,128)} %copy.26.refs_2_, bf16[1792,1024]{1,0:T(8,128)(2,1)} %place_down.3.refs_3_, bf16[512,1024]{1,0:T(8,128)(2,1)} %bitcast.99, f32[512,1]{1,0:T(8,128)} %copy.27.refs_5_), custom_call_target="tpu_custom_call" | custom-call | flops 3758096384 | bytes 11272192 | tf_op jit(solution)/shard_map/down_product/pallas_call | solution.py:246
  258.9 6.1 %collective-permute-done.35 = bf16[2,2,16,1792]{3,2,0,1:T(8,128)(2,1)S(1)} collective-permute-done((bf16[2,2,16,1792]{3,2,0,1:T(8,128)(2,1)S(1)}, bf16[2,2,16,1792]{3,2,0,1:T(8,128)(2,1)S(1)}, u32[]{:S(2)}, u32[]{:S(2)}) %collective-permute-start.35) | collective-permute-done | bytes 229408 | tf_op jit(solution)/shard_map/ppermute | solution.py:262
  266.7 2.5 collective-permute-done.31
  272.1 2.0 collective-permute-done.32
  274.2 2.3 collective-permute-start.33
  277.1 2.2 collective-permute-done.33
  (175 shorter events, 56.8 us)
Async XLA Ops:
  4.0 9.2 %collective-permute-start = (bf16[16,1920]{1,0:T(8,128)(2,1)S(1)}, bf16[16,1920]{1,0:T(8,128)(2,1)S(1)}, u32[]{:S(2)}, u32[]{:S(2)}) collective-permute-start(bf16[16,1920]{1,0:T(8,128)(2,1)S(1)} %fusion.33), channel_id=1, source_target_pairs={{0,1},{1,0},{2,3},{3,2},{4,5},{5,4},{6,7},{7,6},{8,9},{9,8},{10,11... | collective-permute-start | bytes 184328 | tf_op jit(solution)/shard_map/ppermute | solution.py:262
  13.2 71.4 %all-to-all-start = ((bf16[112,128,128]{2,1,0:T(8,128)(2,1)}), bf16[112,128,128]{2,1,0:T(8,128)(2,1)}, u32[]{:S(2)}, u32[]{:S(2)}) async-start(bf16[112,128,128]{2,1,0:T(8,128)(2,1)} %shard_map.95), calls=%async_computation | async-start | bytes 7340032 | tf_op jit(solution)/shard_map/all_to_all | solution.py:353
  17.8 43.0 %collective-permute-start.1 = (bf16[2,16,1920]{2,1,0:T(8,128)(2,1)S(1)}, bf16[2,16,1920]{2,1,0:T(8,128)(2,1)S(1)}, u32[]{:S(2)}, u32[]{:S(2)}) collective-permute-start(bf16[2,16,1920]{2,1,0:T(8,128)(2,1)S(1)} %pad_maximum_fusion.6), channel_id=1, source_target_pairs={{0,16},{2,18},{4,20},{6,22},{8,24},{10,26},{12,28},{14,30},{16,0},... | collective-permute-start | bytes 368648 | tf_op jit(solution)/shard_map/ppermute | solution.py:262
  60.8 11.6 %collective-permute-start.3 = (bf16[2,2,16,1920]{3,2,0,1:T(8,128)(2,1)S(1)}, bf16[2,2,16,1920]{3,2,0,1:T(8,128)(2,1)S(1)}, u32[]{:S(2)}, u32[]{:S(2)}) collective-permute-start(bf16[2,2,16,1920]{3,2,0,1:T(8,128)(2,1)S(1)} %get-tuple-element.105), channel_id=1, source_target_pairs={{0,8},{2,10},{4,12},{6,14},{8,0},{10,2},{12,4},{14,6},{16,24},{18,... | collective-permute-start | bytes 737288 | tf_op jit(solution)/shard_map/ppermute | solution.py:262
  65.6 12.4 %collective-permute-start.2 = (bf16[2,2,16,1920]{3,2,0,1:T(8,128)(2,1)S(1)}, bf16[2,2,16,1920]{3,2,0,1:T(8,128)(2,1)S(1)}, u32[]{:S(2)}, u32[]{:S(2)}) collective-permute-start(bf16[2,2,16,1920]{3,2,0,1:T(8,128)(2,1)S(1)} %get-tuple-element.105), channel_id=1, source_target_pairs={{0,4},{2,6},{4,0},{6,2},{8,12},{10,14},{12,8},{14,10},{16,20},{18,... | collective-permute-start | bytes 737288 | tf_op jit(solution)/shard_map/ppermute | solution.py:262
  67.0 10.9 %collective-permute-start.4 = (bf16[2,2,16,1920]{3,2,0,1:T(8,128)(2,1)S(1)}, bf16[2,2,16,1920]{3,2,0,1:T(8,128)(2,1)S(1)}, u32[]{:S(2)}, u32[]{:S(2)}) collective-permute-start(bf16[2,2,16,1920]{3,2,0,1:T(8,128)(2,1)S(1)} %get-tuple-element.105), channel_id=1, source_target_pairs={{0,12},{2,14},{4,8},{6,10},{8,4},{10,6},{12,0},{14,2},{16,28},{18,... | collective-permute-start | bytes 737288 | tf_op jit(solution)/shard_map/ppermute | solution.py:262
  94.4 13.5 %collective-permute-start.7 = (bf16[1,2,2,64,1024]{4,3,2,1,0:T(8,128)(2,1)S(1)}, bf16[1,2,2,64,1024]{4,3,2,1,0:T(8,128)(2,1)S(1)}, u32[]{:S(2)}, u32[]{:S(2)}) collective-permute-start(bf16[1,2,2,64,1024]{4,3,2,1,0:T(8,128)(2,1)S(1)} %bitcast.101), channel_id=1, source_target_pairs={{0,1},{1,0},{2,3},{3,2},{4,5},{5,4},{6,7},{7,6},{8,9},{9,8},{10,11... | collective-permute-start | bytes 1572872 | tf_op jit(solution)/shard_map/ppermute | solution.py:262
  99.2 10.1 %collective-permute-start.10 = (bf16[7,128,128]{2,1,0:T(8,128)(2,1)}, bf16[7,128,128]{2,1,0:T(8,128)(2,1)S(1)}, u32[]{:S(2)}, u32[]{:S(2)}) collective-permute-start(bf16[7,128,128]{2,1,0:T(8,128)(2,1)} %get-tuple-element.51), channel_id=1, source_target_pairs={{0,4},{2,6},{4,0},{6,2},{8,12},{10,14},{12,8},{14,10},{16,20},{18,... | collective-permute-start | bytes 688136 | tf_op jit(solution)/shard_map/ppermute | solution.py:262
  100.7 11.1 %collective-permute-start.11 = (bf16[7,128,128]{2,1,0:T(8,128)(2,1)}, bf16[7,128,128]{2,1,0:T(8,128)(2,1)S(1)}, u32[]{:S(2)}, u32[]{:S(2)}) collective-permute-start(bf16[7,128,128]{2,1,0:T(8,128)(2,1)} %get-tuple-element.52), channel_id=1, source_target_pairs={{0,6},{2,4},{4,2},{6,0},{8,14},{10,12},{12,10},{14,8},{16,22},{18,... | collective-permute-start | bytes 688136 | tf_op jit(solution)/shard_map/ppermute | solution.py:262
  101.0 12.3 %collective-permute-start.12 = (bf16[7,128,128]{2,1,0:T(8,128)(2,1)}, bf16[7,128,128]{2,1,0:T(8,128)(2,1)S(1)}, u32[]{:S(2)}, u32[]{:S(2)}) collective-permute-start(bf16[7,128,128]{2,1,0:T(8,128)(2,1)} %get-tuple-element.53), channel_id=1, source_target_pairs={{0,8},{2,10},{4,12},{6,14},{8,0},{10,2},{12,4},{14,6},{16,24},{18,... | collective-permute-start | bytes 688136 | tf_op jit(solution)/shard_map/ppermute | solution.py:262
  102.2 18.1 %collective-permute-start.13 = (bf16[7,128,128]{2,1,0:T(8,128)(2,1)}, bf16[7,128,128]{2,1,0:T(8,128)(2,1)S(1)}, u32[]{:S(2)}, u32[]{:S(2)}) collective-permute-start(bf16[7,128,128]{2,1,0:T(8,128)(2,1)} %get-tuple-element.54), channel_id=1, source_target_pairs={{0,10},{2,8},{4,14},{6,12},{8,2},{10,0},{12,6},{14,4},{16,26},{18,... | collective-permute-start | bytes 688136 | tf_op jit(solution)/shard_map/ppermute | solution.py:262
  107.8 24.3 %collective-permute-start.14 = (bf16[7,128,128]{2,1,0:T(8,128)(2,1)}, bf16[7,128,128]{2,1,0:T(8,128)(2,1)S(1)}, u32[]{:S(2)}, u32[]{:S(2)}) collective-permute-start(bf16[7,128,128]{2,1,0:T(8,128)(2,1)} %get-tuple-element.55), channel_id=1, source_target_pairs={{0,12},{2,14},{4,8},{6,10},{8,4},{10,6},{12,0},{14,2},{16,28},{18,... | collective-permute-start | bytes 688136 | tf_op jit(solution)/shard_map/ppermute | solution.py:262
  109.3 63.1 %collective-permute-start.8 = (bf16[1,1,2,64,1024]{4,3,2,1,0:T(8,128)(2,1)S(1)}, bf16[1,1,2,64,1024]{4,3,2,1,0:T(8,128)(2,1)S(1)}, u32[]{:S(2)}, u32[]{:S(2)}) collective-permute-start(bf16[1,1,2,64,1024]{4,3,2,1,0:T(8,128)(2,1)S(1)} %slice.148), channel_id=1, source_target_pairs={{0,16},{2,18},{4,20},{6,22},{8,24},{10,26},{12,28},{14,30},{16,0},... | collective-permute-start | bytes 786440 | tf_op jit(solution)/shard_map/ppermute | solution.py:262
  111.8 26.9 %collective-permute-start.15 = (bf16[7,128,128]{2,1,0:T(8,128)(2,1)}, bf16[7,128,128]{2,1,0:T(8,128)(2,1)S(1)}, u32[]{:S(2)}, u32[]{:S(2)}) collective-permute-start(bf16[7,128,128]{2,1,0:T(8,128)(2,1)} %get-tuple-element.56), channel_id=1, source_target_pairs={{0,14},{2,12},{4,10},{6,8},{8,6},{10,4},{12,2},{14,0},{16,30},{18,... | collective-permute-start | bytes 688136 | tf_op jit(solution)/shard_map/ppermute | solution.py:262
  113.3 26.8 %collective-permute-start.16 = (bf16[7,128,128]{2,1,0:T(8,128)(2,1)}, bf16[7,128,128]{2,1,0:T(8,128)(2,1)S(1)}, u32[]{:S(2)}, u32[]{:S(2)}) collective-permute-start(bf16[7,128,128]{2,1,0:T(8,128)(2,1)} %get-tuple-element.57), channel_id=1, source_target_pairs={{0,16},{2,18},{4,20},{6,22},{8,24},{10,26},{12,28},{14,30},{16,0},... | collective-permute-start | bytes 688136 | tf_op jit(solution)/shard_map/ppermute | solution.py:262
  120.3 36.0 %collective-permute-start.17 = (bf16[7,128,128]{2,1,0:T(8,128)(2,1)}, bf16[7,128,128]{2,1,0:T(8,128)(2,1)S(1)}, u32[]{:S(2)}, u32[]{:S(2)}) collective-permute-start(bf16[7,128,128]{2,1,0:T(8,128)(2,1)} %get-tuple-element.58), channel_id=1, source_target_pairs={{0,18},{2,16},{4,22},{6,20},{8,26},{10,24},{12,30},{14,28},{16,2},... | collective-permute-start | bytes 688136 | tf_op jit(solution)/shard_map/ppermute | solution.py:262
  132.1 38.8 %collective-permute-start.18 = (bf16[7,128,128]{2,1,0:T(8,128)(2,1)}, bf16[7,128,128]{2,1,0:T(8,128)(2,1)}, u32[]{:S(2)}, u32[]{:S(2)}) collective-permute-start(bf16[7,128,128]{2,1,0:T(8,128)(2,1)} %get-tuple-element.59), channel_id=1, source_target_pairs={{0,20},{2,22},{4,16},{6,18},{8,28},{10,30},{12,24},{14,26},{16,4},... | collective-permute-start | bytes 688136 | tf_op jit(solution)/shard_map/ppermute | solution.py:262
  138.7 35.7 %collective-permute-start.19 = (bf16[7,128,128]{2,1,0:T(8,128)(2,1)}, bf16[7,128,128]{2,1,0:T(8,128)(2,1)S(1)}, u32[]{:S(2)}, u32[]{:S(2)}) collective-permute-start(bf16[7,128,128]{2,1,0:T(8,128)(2,1)} %get-tuple-element.60), channel_id=1, source_target_pairs={{0,22},{2,20},{4,18},{6,16},{8,30},{10,28},{12,26},{14,24},{16,6},... | collective-permute-start | bytes 688136 | tf_op jit(solution)/shard_map/ppermute | solution.py:262
  140.1 34.2 %collective-permute-start.20 = (bf16[7,128,128]{2,1,0:T(8,128)(2,1)}, bf16[7,128,128]{2,1,0:T(8,128)(2,1)S(1)}, u32[]{:S(2)}, u32[]{:S(2)}) collective-permute-start(bf16[7,128,128]{2,1,0:T(8,128)(2,1)} %get-tuple-element.61), channel_id=1, source_target_pairs={{0,24},{2,26},{4,28},{6,30},{8,16},{10,18},{12,20},{14,22},{16,8},... | collective-permute-start | bytes 688136 | tf_op jit(solution)/shard_map/ppermute | solution.py:262
  156.3 18.0 %collective-permute-start.21 = (bf16[7,128,128]{2,1,0:T(8,128)(2,1)}, bf16[7,128,128]{2,1,0:T(8,128)(2,1)S(1)}, u32[]{:S(2)}, u32[]{:S(2)}) collective-permute-start(bf16[7,128,128]{2,1,0:T(8,128)(2,1)} %get-tuple-element.62), channel_id=1, source_target_pairs={{0,26},{2,24},{4,30},{6,28},{8,18},{10,16},{12,22},{14,20},{16,10}... | collective-permute-start | bytes 688136 | tf_op jit(solution)/shard_map/ppermute | solution.py:262
  171.0 10.6 %collective-permute-start.22 = (bf16[7,128,128]{2,1,0:T(8,128)(2,1)}, bf16[7,128,128]{2,1,0:T(8,128)(2,1)S(1)}, u32[]{:S(2)}, u32[]{:S(2)}) collective-permute-start(bf16[7,128,128]{2,1,0:T(8,128)(2,1)} %get-tuple-element.63), channel_id=1, source_target_pairs={{0,28},{2,30},{4,24},{6,26},{8,20},{10,22},{12,16},{14,18},{16,12}... | collective-permute-start | bytes 688136 | tf_op jit(solution)/shard_map/ppermute | solution.py:262
  172.4 10.9 %collective-permute-start.23 = (bf16[7,128,128]{2,1,0:T(8,128)(2,1)}, bf16[7,128,128]{2,1,0:T(8,128)(2,1)S(1)}, u32[]{:S(2)}, u32[]{:S(2)}) collective-permute-start(bf16[7,128,128]{2,1,0:T(8,128)(2,1)} %get-tuple-element.64), channel_id=1, source_target_pairs={{0,30},{2,28},{4,26},{6,24},{8,22},{10,20},{12,18},{14,16},{16,14}... | collective-permute-start | bytes 688136 | tf_op jit(solution)/shard_map/ppermute | solution.py:262
  197.1 18.3 %collective-permute-start.27 = (bf16[1,2,1,64,1024]{4,3,2,1,0:T(8,128)(2,1)S(1)}, bf16[1,2,1,64,1024]{4,3,2,1,0:T(8,128)(2,1)S(1)}, u32[]{:S(2)}, u32[]{:S(2)}) collective-permute-start(bf16[1,2,1,64,1024]{4,3,2,1,0:T(8,128)(2,1)S(1)} %slice.152), channel_id=1, source_target_pairs={{0,1},{1,0},{2,3},{3,2},{4,5},{5,4},{6,7},{7,6},{8,9},{9,8},{10,11... | collective-permute-start | bytes 786440 | tf_op jit(solution)/shard_map/ppermute | solution.py:262
  198.6 29.0 %collective-permute-start.24 = (bf16[1,1,2,64,1024]{4,3,2,1,0:T(8,128)(2,1)S(1)}, bf16[1,1,2,64,1024]{4,3,2,1,0:T(8,128)(2,1)S(1)}, u32[]{:S(2)}, u32[]{:S(2)}) collective-permute-start(bf16[1,1,2,64,1024]{4,3,2,1,0:T(8,128)(2,1)S(1)} %multiply_convert_fusion.1), channel_id=1, source_target_pairs={{0,16},{2,18},{4,20},{6,22},{8,24},{10,26},{12,28},{14,30},{16,0},... | collective-permute-start | bytes 786440 | tf_op jit(solution)/shard_map/ppermute | solution.py:262
  215.6 12.9 %collective-permute-start.28 = (bf16[1,2,1,64,1024]{4,3,2,1,0:T(8,128)(2,1)S(1)}, bf16[1,2,1,64,1024]{4,3,2,1,0:T(8,128)(2,1)S(1)}, u32[]{:S(2)}, u32[]{:S(2)}) collective-permute-start(bf16[1,2,1,64,1024]{4,3,2,1,0:T(8,128)(2,1)S(1)} %multiply_convert_fusion), channel_id=1, source_target_pairs={{0,1},{1,0},{2,3},{3,2},{4,5},{5,4},{6,7},{7,6},{8,9},{9,8},{10,11... | collective-permute-start | bytes 786440 | tf_op jit(solution)/shard_map/ppermute | solution.py:262
  227.6 13.4 %collective-permute-start.25 = (bf16[1,2,2,64,1024]{4,3,2,1,0:T(8,128)(2,1)S(1)}, bf16[1,2,2,64,1024]{4,3,2,1,0:T(8,128)(2,1)S(1)}, u32[]{:S(2)}, u32[]{:S(2)}) collective-permute-start(bf16[1,2,2,64,1024]{4,3,2,1,0:T(8,128)(2,1)S(1)} %constant_dynamic-update-slice_fusion), channel_id=1, source_target_pairs={{0,1},{1,0},{2,3},{3,2},{4,5},{5,4},{6,7},{7,6},{8,9},{9,8},{10,11... | collective-permute-start | bytes 1572872 | tf_op jit(solution)/shard_map/ppermute | solution.py:262
  228.5 13.6 %collective-permute-start.29 = (bf16[2,2,1,64,1024]{4,3,2,1,0:T(8,128)(2,1)S(1)}, bf16[2,2,1,64,1024]{4,3,2,1,0:T(8,128)(2,1)S(1)}, u32[]{:S(2)}, u32[]{:S(2)}) collective-permute-start(bf16[2,2,1,64,1024]{4,3,2,1,0:T(8,128)(2,1)S(1)} %pad_maximum_fusion.4), channel_id=1, source_target_pairs={{0,2},{2,0},{4,6},{6,4},{8,10},{10,8},{12,14},{14,12},{16,18},{18,... | collective-permute-start | bytes 1572872 | tf_op jit(solution)/shard_map/ppermute | solution.py:262
  256.5 8.5 %collective-permute-start.35 = (bf16[2,2,16,1792]{3,2,0,1:T(8,128)(2,1)S(1)}, bf16[2,2,16,1792]{3,2,0,1:T(8,128)(2,1)S(1)}, u32[]{:S(2)}, u32[]{:S(2)}) collective-permute-start(bf16[2,2,16,1792]{3,2,0,1:T(8,128)(2,1)S(1)} %slice_bitcast_fusion), channel_id=1, source_target_pairs={{0,8},{2,10},{4,12},{6,14},{8,0},{10,2},{12,4},{14,6},{16,24},{18,... | collective-permute-start | bytes 688136 | tf_op jit(solution)/shard_map/ppermute | solution.py:262
  258.4 10.7 %collective-permute-start.31 = (bf16[2,2,16,1792]{3,2,0,1:T(8,128)(2,1)S(1)}, bf16[2,2,16,1792]{3,2,0,1:T(8,128)(2,1)S(1)}, u32[]{:S(2)}, u32[]{:S(2)}) collective-permute-start(bf16[2,2,16,1792]{3,2,0,1:T(8,128)(2,1)S(1)} %slice_bitcast_fusion.2), channel_id=1, source_target_pairs={{0,8},{2,10},{4,12},{6,14},{8,0},{10,2},{12,4},{14,6},{16,24},{18,... | collective-permute-start | bytes 688136 | tf_op jit(solution)/shard_map/ppermute | solution.py:262
  265.2 5.6 %collective-permute-start.36 = (bf16[2,16,1792]{2,1,0:T(8,128)(2,1)S(1)}, bf16[2,16,1792]{2,1,0:T(8,128)(2,1)S(1)}, u32[]{:S(2)}, u32[]{:S(2)}) collective-permute-start(bf16[2,16,1792]{2,1,0:T(8,128)(2,1)S(1)} %slice_bitcast_fusion.4), channel_id=1, source_target_pairs={{0,4},{2,6},{4,0},{6,2},{8,12},{10,14},{12,8},{14,10},{16,20},{18,... | collective-permute-start | bytes 344072 | tf_op jit(solution)/shard_map/ppermute | solution.py:262
  270.8 5.9 %collective-permute-start.37 = (bf16[16,1792]{1,0:T(8,128)(2,1)S(1)}, bf16[16,1792]{1,0:T(8,128)(2,1)S(1)}, u32[]{:S(2)}, u32[]{:S(2)}) collective-permute-start(bf16[16,1792]{1,0:T(8,128)(2,1)S(1)} %slice_bitcast_fusion.8), channel_id=1, source_target_pairs={{0,16},{2,18},{4,20},{6,22},{8,24},{10,26},{12,28},{14,30},{16,0},... | collective-permute-start | bytes 172040 | tf_op jit(solution)/shard_map/ppermute | solution.py:262
  274.2 5.1 %collective-permute-start.33 = (bf16[16,1792]{1,0:T(8,128)(2,1)S(1)}, bf16[16,1792]{1,0:T(8,128)(2,1)S(1)}, u32[]{:S(2)}, u32[]{:S(2)}) collective-permute-start(bf16[16,1792]{1,0:T(8,128)(2,1)S(1)} %slice_bitcast_fusion.10), channel_id=1, source_target_pairs={{0,16},{2,18},{4,20},{6,22},{8,24},{10,26},{12,28},{14,30},{16,0},... | collective-permute-start | bytes 172040 | tf_op jit(solution)/shard_map/ppermute | solution.py:262
  (31 other events, 449.8 us)

commit v3 on v2

--- a/solution.py
+++ b/solution.py
@@ -127,15 +127,18 @@
     lax.fori_loop(0, rows[1], wait, 0)
 
 
-def up_kernel(step, map_ref, tile_refs, rows_ref, *refs):
-    sources, (out_ref, weight, sems) = refs[:-3], refs[-3:]
+def up_kernel(step, size, map_ref, tile_refs, rows_ref, *refs):
+    sources = refs[:-6]
+    keep_ref, send_ref, rows, weight, rows_sem, sems = refs[-6:]
     tile = sources[0].shape[1:]
     part, width = weight.shape
     row_tiles, col_tiles = part // tile[0], width // tile[1]
+    fetch = pltpu.make_async_copy(rows_ref.at[:, pl.ds(0, part)], rows, rows_sem)
+    fetch.start()
     scatter_tiles(
         0, map_ref, tile_refs, sources, weight, lambda row, column: sems.at[lax.div(column, step)]
     )
-    rows = rows_ref[:, :part]
+    fetch.wait()
     for block in range(col_tiles // step):
         wait_tiles(
             0,
@@ -147,22 +150,28 @@
             range(block * step, block * step + step),
         )
         columns = pl.ds(block * step * tile[1], step * tile[1])
-        out_ref[:, columns] = jnp.dot(
-            rows, weight[:, columns], preferred_element_type=jnp.float32
-        ).astype(out_ref.dtype)
-
-
-def up_product(index, inverse, rows, sources, part, width):
+        product = jnp.dot(
+            rows[...], weight[:, columns], preferred_element_type=jnp.float32
+        ).astype(keep_ref.dtype)
+        for i in range(product.shape[0] // (2 * size)):
+            place = pl.ds(i * size, size)
+            keep_ref[place, columns] = product[2 * i * size : (2 * i + 1) * size]
+            send_ref[place, columns] = product[(2 * i + 1) * size : (2 * i + 2) * size]
+
+
+def up_product(index, inverse, rows, sources, part, width, size):
     tile_cols = sources[0].shape[2]
     step = largest_divisor(width // tile_cols, 4)
     count = rows.shape[0]
     return pl.pallas_call(
-        functools.partial(up_kernel, step),
-        out_shape=jax.ShapeDtypeStruct((count, width), jnp.bfloat16),
-        in_specs=[SMEM, SMEM, VMEM] + [ANY] * len(sources),
-        out_specs=VMEM,
+        functools.partial(up_kernel, step, size),
+        out_shape=[jax.ShapeDtypeStruct((count // 2, width), jnp.bfloat16)] * 2,
+        in_specs=[SMEM, SMEM] + [ANY] * (1 + len(sources)),
+        out_specs=[VMEM, VMEM],
         scratch_shapes=[
+            pltpu.VMEM((count, part), rows.dtype),
             pltpu.VMEM((part, width), sources[0].dtype),
+            pltpu.SemaphoreType.DMA,
             pltpu.SemaphoreType.DMA((width // tile_cols // step,)),
         ],
         cost_estimate=pl.CostEstimate(
@@ -219,36 +228,54 @@
     )(index, inverse, *sources)
 
 
-def down_kernel(*refs):
-    experts = len(refs) // 3
-    out_ref = refs[-1]
+def down_kernel(sizes, split, *refs):
+    experts = len(sizes)
+    outs, held = refs[4 * experts : -1], refs[-1]
+
+    @pl.when(pl.program_id(0) == 0)
+    def _():
+        for e, size in enumerate(sizes):
+            for which in range(2):
+                units = refs[4 * e + 1 + which]
+                for i in range(units.shape[0] // size):
+                    place = pl.ds((2 * i + which) * size, size)
+                    held[e, place, :] = units[pl.ds(i * size, size), :]
+
     total = 0.0
     for e in range(experts):
-        weight, units, factor = refs[3 * e : 3 * e + 3]
+        weight, factor = refs[4 * e], refs[4 * e + 3]
         product = lax.dot_general(
-            units[...], weight[...], (((1,), (1,)), ((), ())), preferred_element_type=jnp.float32
+            held[e], weight[...], (((1,), (1,)), ((), ())), preferred_element_type=jnp.float32
         )
         total = total + product * factor[...]
-    out_ref[...] = total.astype(out_ref.dtype)
-
-
-def down_product(weights, units, factors, block):
+    total = total.astype(outs[0].dtype)
+    count = total.shape[0] // 2
+    for d in range(2):
+        for i in range(count // (2 * split)):
+            for which in range(2):
+                begin = d * count + (2 * i + which) * split
+                outs[2 * d + which][pl.ds(i * split, split), :] = total[begin : begin + split]
+
+
+def down_product(weights, units, sizes, factors, block, split):
     part, width = weights[0].shape
-    count = units[0].shape[0]
+    count = factors[0].shape[0]
     specs, operands = [], []
-    for weight, unit, factor in zip(weights, units, factors, strict=True):
+    for weight, (first, second), factor in zip(weights, units, factors, strict=True):
         specs += [
             pl.BlockSpec((block, width), lambda i: (i, 0)),
-            pl.BlockSpec((count, width), lambda i: (0, 0)),
+            pl.BlockSpec((count // 2, width), lambda i: (0, 0)),
+            pl.BlockSpec((count // 2, width), lambda i: (0, 0)),
             pl.BlockSpec((count, 1), lambda i: (0, 0)),
         ]
-        operands += [weight, unit, factor]
+        operands += [weight, first, second, factor]
     return pl.pallas_call(
-        down_kernel,
+        functools.partial(down_kernel, sizes, split),
         grid=(part // block,),
-        out_shape=jax.ShapeDtypeStruct((count, part), jnp.bfloat16),
+        out_shape=[jax.ShapeDtypeStruct((count // 4, part), jnp.bfloat16)] * 4,
         in_specs=specs,
-        out_specs=pl.BlockSpec((count, block), lambda i: (0, i)),
+        out_specs=[pl.BlockSpec((count // 4, block), lambda i: (0, i))] * 4,
+        scratch_shapes=[pltpu.VMEM((len(weights), count, width), jnp.bfloat16)],
         cost_estimate=pl.CostEstimate(
             flops=2 * len(weights) * count * part * width,
             bytes_accessed=2 * (len(weights) * (part + count) * width + count * part),
@@ -269,22 +296,6 @@
 
 def plain_sum(first, second):
     return (first.astype(jnp.float32) + second.astype(jnp.float32)).astype(jnp.bfloat16)
-
-
-def take(value, axis, which):
-    return lax.index_in_dim(value, which, axis, keepdims=True)
-
-
-def add_up(value, steps):
-    for combine, (axis, name, bit) in steps:
-        value = combine(take(value, axis, 0), flip(take(value, axis, 1), name, bit))
-    return value
-
-
-def gather_back(value, steps):
-    for axis, name, bit in steps:
-        value = jnp.concatenate([value, flip(value, name, bit)], axis=axis)
-    return value
 
 
 def dense_layer(tokens, norm_gain, router, next_router, expert_ids, store, send_list, cache_map):
@@ -349,7 +360,7 @@
         ],
         axis=1,
     )
-    rows, leaving = lax.optimization_barrier((jnp.stack([mine, flip(theirs, *across)]), leaving))
+    rows = jnp.stack([mine, flip(theirs, *across)])
     arrived = lax.all_to_all(
         leaving, "ep", split_axis=0, concat_axis=0, tiled=True, axis_index_groups=groups
     )
@@ -393,37 +404,43 @@
         number = jnp.arange(1, tiles + 1, dtype=jnp.int32)[None, :]
         return jnp.sum(jnp.where(held, number, 0), axis=1) - 1
 
-    shape = (2, 2, 2, half // 2 * tok_dev, hidden_width)
     held_a = (map_a, inverse_of(map_a))
     held_b = (map_b, inverse_of(map_b))
     (map_a, inverse_a), (map_b, inverse_b) = lax.optimization_barrier((held_a, held_b))
-    pre = up_product(map_a, inverse_a, rows, [arrived], part, hidden_width).reshape(shape)
-    own = add_up(pre, [(plain_sum, (0,) + across)])
+    quarter = half * tok_dev
+    keep, send = up_product(map_a, inverse_a, rows, [arrived], part, hidden_width, 2 * quarter)
+    own = plain_sum(keep, flip(send, *across))
     down_a = place_down(map_a, inverse_a, tiles // 2, [arrived], part, hidden_width)
-    own = silu_sum(take(own, 1, 0), flip(take(own, 1, 1), *mirror))
-    kept, crossed, down_a = lax.optimization_barrier((own, crossed, down_a))
-    units_a = jnp.concatenate([kept, flip(own, *mirror)], axis=1)
-    units_a = gather_back(units_a, [(0,) + across])
-    pre = up_product(map_b, inverse_b, rows, crossed, part, hidden_width).reshape(shape)
-    own = add_up(pre, [(plain_sum, (2,) + beside), (silu_sum, (0,) + across)])
-    units_b = gather_back(own, [(0,) + across, (2,) + beside])
+    own = silu_sum(own[:quarter], flip(own[quarter:], *mirror))
+    kept, crossed, down_a, factors = lax.optimization_barrier((own, crossed, down_a, factors))
+    own = jnp.concatenate([kept, flip(own, *across)], axis=0)
+    units_a = (own, flip(own, *mirror))
+
+    eighth = half // 2 * tok_dev
+    keep, send = up_product(map_b, inverse_b, rows, crossed, part, hidden_width, eighth)
+    own = plain_sum(keep, flip(send, *beside))
+    own = silu_sum(own[:quarter], flip(own[quarter:], *across))
+    own = jnp.concatenate([own, flip(own, *across)], axis=0)
+    units_b = (own, flip(own, *beside))
     down_b = place_down(map_b, inverse_b, tiles // 2, crossed, part, hidden_width)
-    flat = (2 * n_ep * tok_dev, hidden_width)
-    units = [units_a.reshape(flat), units_b.reshape(flat)]
-    product = down_product(
-        [down_a, down_b], units, factors, tile_rows * largest_divisor(row_tiles, 2)
-    )
-    bits = [half]
-    while bits[0] > 1:
-        bits.insert(0, bits[0] // 2)
-    bits = [bits[0]] + bits[-2:0:-1] + [bits[-1]]
-    product = product.reshape((2, 2) + (2,) * (len(bits) - 1) + (tok_dev, part))
+
+    products = down_product(
+        [down_a, down_b],
+        [units_a, units_b],
+        (quarter, eighth),
+        factors,
+        tile_rows * largest_divisor(row_tiles, 2),
+        eighth,
+    )
     sums = [None, None]
     for d in (1, 0):
-        total = product[d]
-        for bit in bits[:-1]:
-            total = plain_sum(total[:, 0], flip(total[:, 1], "ep", bit))
-        sums[d] = plain_sum(total[0], flip(total[1], "ep", bits[-1]))
+        total = plain_sum(products[2 * d], flip(products[2 * d + 1], *beside))
+        total = total.reshape(2, half // 2, tok_dev, part)
+        pieces = [total[:, 0]]
+        for m in range(1, half // 2):
+            pieces.append(flip(total[:, m], "ep", 2 * m))
+        total = sum(piece.astype(jnp.float32) for piece in pieces).astype(jnp.bfloat16)
+        sums[d] = plain_sum(total[0], flip(total[1], *mirror))
     mine, other = sums[0], flip(sums[1], *across)
     mixed = jnp.where(
         side == 0,

time: 283 us -> 282 us (level)
  starting transfers between devices: 64.7 us -> 76.3 us
  waiting for transfers between devices: 150 us -> 146 us
  other arithmetic: 11.3 us -> 7.57 us
  local copies, waits for them, and re-layouts: 8.77 us -> 5.6 us
    ppermute x39 -> x41, starting transfers between devices: 60.2 us -> 70.9 us  [flip(): lax.ppermute(value, axis, [(i, i ^ bit) for i in range(lax.axis_size(axis...]
    ppermute x39 -> x41, waiting for transfers between devices: 150 us -> 146 us  [flip(): lax.ppermute(value, axis, [(i, i ^ bit) for i in range(lax.axis_size(axis...]
    slice x7 -> x2, local copies, waits for them, and re-layouts: 4.09 us -> 0.04 us  [the longest x1 0.02 us: dense_layer(): own = silu_sum(own[:quarter], flip(own[quarter:], *mirror))]
  transfers between devices with their start and end apart: 40 -> 42, of which waited for: 24 -> 29; matrix products, arithmetic and copies ran while one was open for 3% -> 3% of each run, Pallas kernels for 7% -> 5%
where the time goes in v3:
time: 282 us; the launch traced here: 281 us
  waiting for transfers between devices  146 us (52%)
  starting transfers between devices  76.3 us (27%)
  Pallas kernels  43.2 us (15%)
  other arithmetic  7.57 us (3%)
  local copies, waits for them, and re-layouts  5.6 us (2%)
    ppermute x41, waiting for transfers between devices, flip(): lax.ppermute(value, axis, [(i, i ^ bit) for i in range(lax.axis_size(axis...  146 us
    ppermute x41, starting transfers between devices, flip(): lax.ppermute(value, axis, [(i, i ^ bit) for i in range(lax.axis_size(axis...  70.9 us
    pallas_call x2, Pallas kernels, up_product(): pl.pallas_call(functools.partial(up_kernel, step, size), out_shape=[jax.S...  14.5 us
    pallas_call x2, Pallas kernels, place_down(): pl.pallas_call(functools.partial(place_kernel, first, chunks), out_shape=...  10.8 us
    pallas_call x1, Pallas kernels, down_product(): pl.pallas_call(functools.partial(down_kernel, sizes, split), grid=(part /...  9.57 us
    pallas_call x2, Pallas kernels, pick_tiles(): pl.pallas_call(functools.partial(pick_kernel, column_of, chunks, size), o...  8.34 us
  transfers between devices with their start and end apart: 42, of which 29 were waited for; matrix products, arithmetic and copies ran while one was open for 3% of the time, Pallas kernels for 5%

profile of v3, /device:TPU:0, one launch (start us, length us, event | category | flops | bytes accessed | tf_op | source)
XLA Modules:
  0.0 281.2 jit_solution(18144619872500450423)
XLA Ops:
  0.7 4.2 %shard_map.95 = bf16[112,128,128]{2,1,0:T(8,128)(2,1)} custom-call(s32[1]{0:T(128)} %bitcast.11.place_ref, s32[224]{0:T(256)} %bitcast.94, bf16[224,128,128]{2,1,0:T(8,128)(2,1)} %bitcast.76), custom_call_target="tpu_custom_call" | custom-call | flops 1879048192 | bytes 14680064 | tf_op jit(solution)/shard_map/pallas_call | solution.py:51
  4.9 5.4 %all-to-all-start = ((bf16[112,128,128]{2,1,0:T(8,128)(2,1)}), bf16[112,128,128]{2,1,0:T(8,128)(2,1)}, u32[]{:S(2)}, u32[]{:S(2)}) async-start(bf16[112,128,128]{2,1,0:T(8,128)(2,1)} %shard_map.95), calls=%async_computation | async-start | bytes 7340032 | tf_op jit(solution)/shard_map/all_to_all | solution.py:364
  11.2 2.3 collective-permute-start
  16.1 2.9 %collective-permute-start.1 = (bf16[2,16,1920]{2,1,0:T(8,128)(2,1)S(1)}, bf16[2,16,1920]{2,1,0:T(8,128)(2,1)S(1)}, u32[]{:S(2)}, u32[]{:S(2)}) collective-permute-start(bf16[2,16,1920]{2,1,0:T(8,128)(2,1)S(1)} %get-tuple-element.121), channel_id=1, source_target_pairs={{0,16},{2,18},{4,20},{6,22},{8,24},{10,26},{12,28},{14,30},{16,0},... | collective-permute-start | bytes 368648 | tf_op jit(solution)/shard_map/ppermute | solution.py:289
  19.0 34.5 %collective-permute-done.1 = bf16[2,16,1920]{2,1,0:T(8,128)(2,1)S(1)} collective-permute-done((bf16[2,16,1920]{2,1,0:T(8,128)(2,1)S(1)}, bf16[2,16,1920]{2,1,0:T(8,128)(2,1)S(1)}, u32[]{:S(2)}, u32[]{:S(2)}) %collective-permute-start.1) | collective-permute-done | bytes 122912 | tf_op jit(solution)/shard_map/ppermute | solution.py:289
  55.2 5.1 %collective-permute-start.3 = (bf16[2,2,16,1920]{3,2,0,1:T(8,128)(2,1)S(1)}, bf16[2,2,16,1920]{3,2,0,1:T(8,128)(2,1)S(1)}, u32[]{:S(2)}, u32[]{:S(2)}) collective-permute-start(bf16[2,2,16,1920]{3,2,0,1:T(8,128)(2,1)S(1)} %get-tuple-element.119), channel_id=1, source_target_pairs={{0,8},{2,10},{4,12},{6,14},{8,0},{10,2},{12,4},{14,6},{16,24},{18,... | collective-permute-start | bytes 737288 | tf_op jit(solution)/shard_map/ppermute | solution.py:289
  61.3 5.8 %collective-permute-done.3 = bf16[2,2,16,1920]{3,2,0,1:T(8,128)(2,1)S(1)} collective-permute-done((bf16[2,2,16,1920]{3,2,0,1:T(8,128)(2,1)S(1)}, bf16[2,2,16,1920]{3,2,0,1:T(8,128)(2,1)S(1)}, u32[]{:S(2)}, u32[]{:S(2)}) %collective-permute-start.3) | collective-permute-done | bytes 245792 | tf_op jit(solution)/shard_map/ppermute | solution.py:289
  67.1 3.8 %collective-permute-done.4 = bf16[2,2,16,1920]{3,2,0,1:T(8,128)(2,1)S(1)} collective-permute-done((bf16[2,2,16,1920]{3,2,0,1:T(8,128)(2,1)S(1)}, bf16[2,2,16,1920]{3,2,0,1:T(8,128)(2,1)S(1)}, u32[]{:S(2)}, u32[]{:S(2)}) %collective-permute-start.4) | collective-permute-done | bytes 245792 | tf_op jit(solution)/shard_map/ppermute | solution.py:289
  77.7 7.3 %up_product.2 = (bf16[256,1024]{1,0:T(8,128)(2,1)}, bf16[256,1024]{1,0:T(8,128)(2,1)}) custom-call(s32[224]{0:T(256)} %copy-done.23, s32[112]{0:T(128)} %broadcast_add_fusion.1.tile_refs, bf16[512,1920]{1,0:T(8,128)(2,1)} %bitcast.79, bf16[112,128,128]{2,1,0:T(8,128)(2,1)} %all-to-all-done.refs_0_), custom_call_target="tpu_custom_call" | custom-call | flops 1879048192 | bytes 6553600 | tf_op jit(solution)/shard_map/up_product/pallas_call | solution.py:166
  86.6 4.1 %shard_map.96 = (bf16[7,128,128]{2,1,0:T(8,128)(2,1)}, bf16[7,128,128]{2,1,0:T(8,128)(2,1)}, bf16[7,128,128]{2,1,0:T(8,128)(2,1)}, bf16[7,128,128]{2,1,0:T(8,128...) custom-call(s32[1]{0:T(128)} %bitcast.11.place_ref, ...), custom_call_target="tpu_custom_call" | custom-call | flops 1879048192 | bytes 14680064 | tf_op jit(solution)/shard_map/pallas_call | solution.py:51
  94.3 5.2 %collective-permute-done.10.refs_2_ = bf16[7,128,128]{2,1,0:T(8,128)(2,1)S(1)} collective-permute-done((bf16[7,128,128]{2,1,0:T(8,128)(2,1)}, bf16[7,128,128]{2,1,0:T(8,128)(2,1)S(1)}, u32[]{:S(2)}, u32[]{:S(2)}) %collective-permute-start.10) | collective-permute-done | bytes 229408 | tf_op jit(solution)/shard_map/ppermute | solution.py:289
  99.5 2.7 collective-permute-start.14
  102.5 2.6 collective-permute-start.17
  107.1 12.1 %collective-permute-done.14.refs_6_ = bf16[7,128,128]{2,1,0:T(8,128)(2,1)S(1)} collective-permute-done((bf16[7,128,128]{2,1,0:T(8,128)(2,1)}, bf16[7,128,128]{2,1,0:T(8,128)(2,1)S(1)}, u32[]{:S(2)}, u32[]{:S(2)}) %collective-permute-start.14) | collective-permute-done | bytes 229408 | tf_op jit(solution)/shard_map/ppermute | solution.py:289
  119.1 2.4 collective-permute-start.19
  121.6 3.0 %collective-permute-done.15.refs_7_ = bf16[7,128,128]{2,1,0:T(8,128)(2,1)S(1)} collective-permute-done((bf16[7,128,128]{2,1,0:T(8,128)(2,1)}, bf16[7,128,128]{2,1,0:T(8,128)(2,1)S(1)}, u32[]{:S(2)}, u32[]{:S(2)}) %collective-permute-start.15) | collective-permute-done | bytes 229408 | tf_op jit(solution)/shard_map/ppermute | solution.py:289
  126.7 5.8 %place_down.2.refs_0_ = bf16[1792,1024]{1,0:T(8,128)(2,1)} custom-call(s32[224]{0:T(256)} %copy-done.23, s32[112]{0:T(128)} %broadcast_add_fusion.1.tile_refs, bf16[112,128,128]{2,1,0:T(8,128)(2,1)} %all-to-all-done.refs_0_), custom_call_target="tpu_custom_call" | custom-call | flops 1879048192 | bytes 7340032 | tf_op jit(solution)/shard_map/place_down/pallas_call | solution.py:214
  132.6 2.6 collective-permute-start.20
  135.2 10.9 %collective-permute-done.17.refs_9_ = bf16[7,128,128]{2,1,0:T(8,128)(2,1)S(1)} collective-permute-done((bf16[7,128,128]{2,1,0:T(8,128)(2,1)}, bf16[7,128,128]{2,1,0:T(8,128)(2,1)S(1)}, u32[]{:S(2)}, u32[]{:S(2)}) %collective-permute-start.17) | collective-permute-done | bytes 229408 | tf_op jit(solution)/shard_map/ppermute | solution.py:289
  146.0 5.8 %collective-permute-done.18.refs_10_ = bf16[7,128,128]{2,1,0:T(8,128)(2,1)} collective-permute-done((bf16[7,128,128]{2,1,0:T(8,128)(2,1)}, bf16[7,128,128]{2,1,0:T(8,128)(2,1)}, u32[]{:S(2)}, u32[]{:S(2)}) %collective-permute-start.18) | collective-permute-done | bytes 229408 | tf_op jit(solution)/shard_map/ppermute | solution.py:289
  151.9 6.4 %collective-permute-start.22 = (bf16[7,128,128]{2,1,0:T(8,128)(2,1)}, bf16[7,128,128]{2,1,0:T(8,128)(2,1)S(1)}, u32[]{:S(2)}, u32[]{:S(2)}) collective-permute-start(bf16[7,128,128]{2,1,0:T(8,128)(2,1)} %get-tuple-element.71), channel_id=1, source_target_pairs={{0,28},{2,30},{4,24},{6,26},{8,20},{10,22},{12,16},{14,18},{16,12}... | collective-permute-start | bytes 688136 | tf_op jit(solution)/shard_map/ppermute | solution.py:289
  158.3 9.0 %collective-permute-done.19.refs_11_ = bf16[7,128,128]{2,1,0:T(8,128)(2,1)} collective-permute-done((bf16[7,128,128]{2,1,0:T(8,128)(2,1)}, bf16[7,128,128]{2,1,0:T(8,128)(2,1)}, u32[]{:S(2)}, u32[]{:S(2)}) %collective-permute-start.19) | collective-permute-done | bytes 229408 | tf_op jit(solution)/shard_map/ppermute | solution.py:289
  167.3 10.1 %collective-permute-done.8 = bf16[128,1024]{1,0:T(8,128)(2,1)S(1)} collective-permute-done((bf16[128,1024]{1,0:T(8,128)(2,1)S(1)}, bf16[128,1024]{1,0:T(8,128)(2,1)S(1)}, u32[]{:S(2)}, u32[]{:S(2)}) %collective-permute-start.8) | collective-permute-done | bytes 262176 | tf_op jit(solution)/shard_map/ppermute | solution.py:289
  179.8 7.1 %up_product.3 = (bf16[256,1024]{1,0:T(8,128)(2,1)}, bf16[256,1024]{1,0:T(8,128)(2,1)}) custom-call(s32[224]{0:T(256)} %copy-done.22, s32[112]{0:T(128)} %broadcast_add_fusion.tile_refs, bf16[512,1920]{1,0:T(8,128)(2,1)} %bitcast.81, bf16[7,128,128]{2,1,0:T(8,128)(2,1)} %get-tuple-element.78.refs_0_, bf16[7,128,128]{2,1,0:T(8,128)(2,1)} %copy-done.18, ...), custom_call_target="tpu_custom_call" | custom-call | flops 1879048192 | bytes 6553600 | tf_op jit(solution)/shard_map/up_product/pallas_call | solution.py:166
  192.5 7.1 %collective-permute-done.27 = bf16[128,1024]{1,0:T(8,128)(2,1)S(1)} collective-permute-done((bf16[128,1024]{1,0:T(8,128)(2,1)S(1)}, bf16[128,1024]{1,0:T(8,128)(2,1)S(1)}, u32[]{:S(2)}, u32[]{:S(2)}) %collective-permute-start.27) | collective-permute-done | bytes 262176 | tf_op jit(solution)/shard_map/ppermute | solution.py:289
  200.4 4.8 %collective-permute-done.24 = bf16[128,1024]{1,0:T(8,128)(2,1)S(1)} collective-permute-done((bf16[128,1024]{1,0:T(8,128)(2,1)S(1)}, bf16[128,1024]{1,0:T(8,128)(2,1)S(1)}, u32[]{:S(2)}, u32[]{:S(2)}) %collective-permute-start.24) | collective-permute-done | bytes 262176 | tf_op jit(solution)/shard_map/ppermute | solution.py:289
  205.3 17.8 %collective-permute-start.25 = (bf16[256,1024]{1,0:T(8,128)(2,1)S(1)}, bf16[256,1024]{1,0:T(8,128)(2,1)S(1)}, u32[]{:S(2)}, u32[]{:S(2)}) collective-permute-start(bf16[256,1024]{1,0:T(8,128)(2,1)S(1)} %constant_dynamic-update-slice_fusion.refs_1_), channel_id=1, source_target_pairs={{0,16},{2,18},{4,20},{6,22},{8,24},{10,26},{12,28},{14,30},{16,0},... | collective-permute-start | bytes 1572872 | tf_op jit(solution)/shard_map/ppermute | solution.py:289
  225.0 5.0 %place_down.3.refs_4_ = bf16[1792,1024]{1,0:T(8,128)(2,1)} custom-call(s32[224]{0:T(256)} %copy-done.22, s32[112]{0:T(128)} %broadcast_add_fusion.tile_refs, bf16[7,128,128]{2,1,0:T(8,128)(2,1)} %get-tuple-element.78.refs_0_, bf16[7,128,128]{2,1,0:T(8,128)(2,1)} %copy-done.18, bf16[7,128,128]{2,1,0:T(8,128)(2,1)} %copy-done.6, ...), custom_call_target="tpu_custom_call" | custom-call | flops 1879048192 | bytes 7340032 | tf_op jit(solution)/shard_map/place_down/pallas_call | solution.py:214
  230.0 14.9 %collective-permute-done.25.refs_2_ = bf16[256,1024]{1,0:T(8,128)(2,1)S(1)} collective-permute-done((bf16[256,1024]{1,0:T(8,128)(2,1)S(1)}, bf16[256,1024]{1,0:T(8,128)(2,1)S(1)}, u32[]{:S(2)}, u32[]{:S(2)}) %collective-permute-start.25) | collective-permute-done | bytes 524320 | tf_op jit(solution)/shard_map/ppermute | solution.py:289
  246.5 9.6 %down_product.1 = (bf16[128,1792]{1,0:T(8,128)(2,1)}, bf16[128,1792]{1,0:T(8,128)(2,1)}, bf16[128,1792]{1,0:T(8,128)(2,1)}, bf16[128,1792]{1,0:T(8,128)(2,1)}) custom-call(bf16[1792,1024]{1,0:T(8,128)(2,1)} %place_down.2.refs_0_, bf16[256,1024]{1,0:T(8,128)(2,1)} %copy-done.19, bf16[256,1024]{1,0:T(8,128)(2,1)} %copy-done.26, f32[512,1]{1,0:T(8,128)} %copy.34.refs_3_, ...), custom_call_target="tpu_custom_call" | custom-call | flops 3758096384 | bytes 11272192 | tf_op jit(solution)/shard_map/down_product/pallas_call | solution.py:272
  266.7 2.6 collective-permute-done.38
  276.5 3.1 %collective-permute-done.34 = bf16[16,1792]{1,0:T(8,128)(2,1)S(1)} collective-permute-done((bf16[16,1792]{1,0:T(8,128)(2,1)S(1)}, bf16[16,1792]{1,0:T(8,128)(2,1)S(1)}, u32[]{:S(2)}, u32[]{:S(2)}) %collective-permute-start.34) | collective-permute-done | bytes 57376 | tf_op jit(solution)/shard_map/ppermute | solution.py:289
  (178 shorter events, 53.7 us)
Async XLA Ops:
  4.9 72.8 %all-to-all-start = ((bf16[112,128,128]{2,1,0:T(8,128)(2,1)}), bf16[112,128,128]{2,1,0:T(8,128)(2,1)}, u32[]{:S(2)}, u32[]{:S(2)}) async-start(bf16[112,128,128]{2,1,0:T(8,128)(2,1)} %shard_map.95), calls=%async_computation | async-start | bytes 7340032 | tf_op jit(solution)/shard_map/all_to_all | solution.py:364
  16.1 37.4 %collective-permute-start.1 = (bf16[2,16,1920]{2,1,0:T(8,128)(2,1)S(1)}, bf16[2,16,1920]{2,1,0:T(8,128)(2,1)S(1)}, u32[]{:S(2)}, u32[]{:S(2)}) collective-permute-start(bf16[2,16,1920]{2,1,0:T(8,128)(2,1)S(1)} %get-tuple-element.121), channel_id=1, source_target_pairs={{0,16},{2,18},{4,20},{6,22},{8,24},{10,26},{12,28},{14,30},{16,0},... | collective-permute-start | bytes 368648 | tf_op jit(solution)/shard_map/ppermute | solution.py:289
  53.5 7.9 %collective-permute-start.2 = (bf16[2,2,16,1920]{3,2,0,1:T(8,128)(2,1)S(1)}, bf16[2,2,16,1920]{3,2,0,1:T(8,128)(2,1)S(1)}, u32[]{:S(2)}, u32[]{:S(2)}) collective-permute-start(bf16[2,2,16,1920]{3,2,0,1:T(8,128)(2,1)S(1)} %get-tuple-element.119), channel_id=1, source_target_pairs={{0,4},{2,6},{4,0},{6,2},{8,12},{10,14},{12,8},{14,10},{16,20},{18,... | collective-permute-start | bytes 737288 | tf_op jit(solution)/shard_map/ppermute | solution.py:289
  55.2 11.9 %collective-permute-start.3 = (bf16[2,2,16,1920]{3,2,0,1:T(8,128)(2,1)S(1)}, bf16[2,2,16,1920]{3,2,0,1:T(8,128)(2,1)S(1)}, u32[]{:S(2)}, u32[]{:S(2)}) collective-permute-start(bf16[2,2,16,1920]{3,2,0,1:T(8,128)(2,1)S(1)} %get-tuple-element.119), channel_id=1, source_target_pairs={{0,8},{2,10},{4,12},{6,14},{8,0},{10,2},{12,4},{14,6},{16,24},{18,... | collective-permute-start | bytes 737288 | tf_op jit(solution)/shard_map/ppermute | solution.py:289
  60.3 10.6 %collective-permute-start.4 = (bf16[2,2,16,1920]{3,2,0,1:T(8,128)(2,1)S(1)}, bf16[2,2,16,1920]{3,2,0,1:T(8,128)(2,1)S(1)}, u32[]{:S(2)}, u32[]{:S(2)}) collective-permute-start(bf16[2,2,16,1920]{3,2,0,1:T(8,128)(2,1)S(1)} %get-tuple-element.119), channel_id=1, source_target_pairs={{0,12},{2,14},{4,8},{6,10},{8,4},{10,6},{12,0},{14,2},{16,28},{18,... | collective-permute-start | bytes 737288 | tf_op jit(solution)/shard_map/ppermute | solution.py:289
  85.0 17.1 %collective-permute-start.7 = (bf16[256,1024]{1,0:T(8,128)(2,1)}, bf16[256,1024]{1,0:T(8,128)(2,1)S(1)}, u32[]{:S(2)}, u32[]{:S(2)}) collective-permute-start(bf16[256,1024]{1,0:T(8,128)(2,1)} %get-tuple-element.56), channel_id=1, source_target_pairs={{0,1},{1,0},{2,3},{3,2},{4,5},{5,4},{6,7},{7,6},{8,9},{9,8},{10,11... | collective-permute-start | bytes 1572872 | tf_op jit(solution)/shard_map/ppermute | solution.py:289
  90.7 8.8 %collective-permute-start.10 = (bf16[7,128,128]{2,1,0:T(8,128)(2,1)}, bf16[7,128,128]{2,1,0:T(8,128)(2,1)S(1)}, u32[]{:S(2)}, u32[]{:S(2)}) collective-permute-start(bf16[7,128,128]{2,1,0:T(8,128)(2,1)} %get-tuple-element.59), channel_id=1, source_target_pairs={{0,4},{2,6},{4,0},{6,2},{8,12},{10,14},{12,8},{14,10},{16,20},{18,... | collective-permute-start | bytes 688136 | tf_op jit(solution)/shard_map/ppermute | solution.py:289
  92.3 10.1 %collective-permute-start.11 = (bf16[7,128,128]{2,1,0:T(8,128)(2,1)}, bf16[7,128,128]{2,1,0:T(8,128)(2,1)S(1)}, u32[]{:S(2)}, u32[]{:S(2)}) collective-permute-start(bf16[7,128,128]{2,1,0:T(8,128)(2,1)} %get-tuple-element.60), channel_id=1, source_target_pairs={{0,6},{2,4},{4,2},{6,0},{8,14},{10,12},{12,10},{14,8},{16,22},{18,... | collective-permute-start | bytes 688136 | tf_op jit(solution)/shard_map/ppermute | solution.py:289
  92.3 10.2 %collective-permute-start.12 = (bf16[7,128,128]{2,1,0:T(8,128)(2,1)}, bf16[7,128,128]{2,1,0:T(8,128)(2,1)S(1)}, u32[]{:S(2)}, u32[]{:S(2)}) collective-permute-start(bf16[7,128,128]{2,1,0:T(8,128)(2,1)} %get-tuple-element.61), channel_id=1, source_target_pairs={{0,8},{2,10},{4,12},{6,14},{8,0},{10,2},{12,4},{14,6},{16,24},{18,... | collective-permute-start | bytes 688136 | tf_op jit(solution)/shard_map/ppermute | solution.py:289
  94.0 11.3 %collective-permute-start.13 = (bf16[7,128,128]{2,1,0:T(8,128)(2,1)}, bf16[7,128,128]{2,1,0:T(8,128)(2,1)S(1)}, u32[]{:S(2)}, u32[]{:S(2)}) collective-permute-start(bf16[7,128,128]{2,1,0:T(8,128)(2,1)} %get-tuple-element.62), channel_id=1, source_target_pairs={{0,10},{2,8},{4,14},{6,12},{8,2},{10,0},{12,6},{14,4},{16,26},{18,... | collective-permute-start | bytes 688136 | tf_op jit(solution)/shard_map/ppermute | solution.py:289
  99.5 19.7 %collective-permute-start.14 = (bf16[7,128,128]{2,1,0:T(8,128)(2,1)}, bf16[7,128,128]{2,1,0:T(8,128)(2,1)S(1)}, u32[]{:S(2)}, u32[]{:S(2)}) collective-permute-start(bf16[7,128,128]{2,1,0:T(8,128)(2,1)} %get-tuple-element.63), channel_id=1, source_target_pairs={{0,12},{2,14},{4,8},{6,10},{8,4},{10,6},{12,0},{14,2},{16,28},{18,... | collective-permute-start | bytes 688136 | tf_op jit(solution)/shard_map/ppermute | solution.py:289
  102.1 22.5 %collective-permute-start.15 = (bf16[7,128,128]{2,1,0:T(8,128)(2,1)}, bf16[7,128,128]{2,1,0:T(8,128)(2,1)S(1)}, u32[]{:S(2)}, u32[]{:S(2)}) collective-permute-start(bf16[7,128,128]{2,1,0:T(8,128)(2,1)} %get-tuple-element.64), channel_id=1, source_target_pairs={{0,14},{2,12},{4,10},{6,8},{8,6},{10,4},{12,2},{14,0},{16,30},{18,... | collective-permute-start | bytes 688136 | tf_op jit(solution)/shard_map/ppermute | solution.py:289
  102.4 30.2 %collective-permute-start.16 = (bf16[7,128,128]{2,1,0:T(8,128)(2,1)}, bf16[7,128,128]{2,1,0:T(8,128)(2,1)S(1)}, u32[]{:S(2)}, u32[]{:S(2)}) collective-permute-start(bf16[7,128,128]{2,1,0:T(8,128)(2,1)} %get-tuple-element.65), channel_id=1, source_target_pairs={{0,16},{2,18},{4,20},{6,22},{8,24},{10,26},{12,28},{14,30},{16,0},... | collective-permute-start | bytes 688136 | tf_op jit(solution)/shard_map/ppermute | solution.py:289
  102.5 43.5 %collective-permute-start.17 = (bf16[7,128,128]{2,1,0:T(8,128)(2,1)}, bf16[7,128,128]{2,1,0:T(8,128)(2,1)S(1)}, u32[]{:S(2)}, u32[]{:S(2)}) collective-permute-start(bf16[7,128,128]{2,1,0:T(8,128)(2,1)} %get-tuple-element.66), channel_id=1, source_target_pairs={{0,18},{2,16},{4,22},{6,20},{8,26},{10,24},{12,30},{14,28},{16,2},... | collective-permute-start | bytes 688136 | tf_op jit(solution)/shard_map/ppermute | solution.py:289
  105.3 46.6 %collective-permute-start.18 = (bf16[7,128,128]{2,1,0:T(8,128)(2,1)}, bf16[7,128,128]{2,1,0:T(8,128)(2,1)}, u32[]{:S(2)}, u32[]{:S(2)}) collective-permute-start(bf16[7,128,128]{2,1,0:T(8,128)(2,1)} %get-tuple-element.67), channel_id=1, source_target_pairs={{0,20},{2,22},{4,16},{6,18},{8,28},{10,30},{12,24},{14,26},{16,4},... | collective-permute-start | bytes 688136 | tf_op jit(solution)/shard_map/ppermute | solution.py:289
  119.1 48.1 %collective-permute-start.19 = (bf16[7,128,128]{2,1,0:T(8,128)(2,1)}, bf16[7,128,128]{2,1,0:T(8,128)(2,1)}, u32[]{:S(2)}, u32[]{:S(2)}) collective-permute-start(bf16[7,128,128]{2,1,0:T(8,128)(2,1)} %get-tuple-element.68), channel_id=1, source_target_pairs={{0,22},{2,20},{4,18},{6,16},{8,30},{10,28},{12,26},{14,24},{16,6},... | collective-permute-start | bytes 688136 | tf_op jit(solution)/shard_map/ppermute | solution.py:289
  124.6 52.8 %collective-permute-start.8 = (bf16[128,1024]{1,0:T(8,128)(2,1)S(1)}, bf16[128,1024]{1,0:T(8,128)(2,1)S(1)}, u32[]{:S(2)}, u32[]{:S(2)}) collective-permute-start(bf16[128,1024]{1,0:T(8,128)(2,1)S(1)} %slice.99), channel_id=1, source_target_pairs={{0,16},{2,18},{4,20},{6,22},{8,24},{10,26},{12,28},{14,30},{16,0},... | collective-permute-start | bytes 786440 | tf_op jit(solution)/shard_map/ppermute | solution.py:289
  132.6 45.0 %collective-permute-start.20 = (bf16[7,128,128]{2,1,0:T(8,128)(2,1)}, bf16[7,128,128]{2,1,0:T(8,128)(2,1)S(1)}, u32[]{:S(2)}, u32[]{:S(2)}) collective-permute-start(bf16[7,128,128]{2,1,0:T(8,128)(2,1)} %get-tuple-element.69), channel_id=1, source_target_pairs={{0,24},{2,26},{4,28},{6,30},{8,16},{10,18},{12,20},{14,22},{16,8},... | collective-permute-start | bytes 688136 | tf_op jit(solution)/shard_map/ppermute | solution.py:289
  146.0 31.6 %collective-permute-start.21 = (bf16[7,128,128]{2,1,0:T(8,128)(2,1)}, bf16[7,128,128]{2,1,0:T(8,128)(2,1)S(1)}, u32[]{:S(2)}, u32[]{:S(2)}) collective-permute-start(bf16[7,128,128]{2,1,0:T(8,128)(2,1)} %get-tuple-element.70), channel_id=1, source_target_pairs={{0,26},{2,24},{4,30},{6,28},{8,18},{10,16},{12,22},{14,20},{16,10}... | collective-permute-start | bytes 688136 | tf_op jit(solution)/shard_map/ppermute | solution.py:289
  151.9 25.7 %collective-permute-start.22 = (bf16[7,128,128]{2,1,0:T(8,128)(2,1)}, bf16[7,128,128]{2,1,0:T(8,128)(2,1)S(1)}, u32[]{:S(2)}, u32[]{:S(2)}) collective-permute-start(bf16[7,128,128]{2,1,0:T(8,128)(2,1)} %get-tuple-element.71), channel_id=1, source_target_pairs={{0,28},{2,30},{4,24},{6,26},{8,20},{10,22},{12,16},{14,18},{16,12}... | collective-permute-start | bytes 688136 | tf_op jit(solution)/shard_map/ppermute | solution.py:289
  167.3 10.5 %collective-permute-start.23 = (bf16[7,128,128]{2,1,0:T(8,128)(2,1)}, bf16[7,128,128]{2,1,0:T(8,128)(2,1)S(1)}, u32[]{:S(2)}, u32[]{:S(2)}) collective-permute-start(bf16[7,128,128]{2,1,0:T(8,128)(2,1)} %get-tuple-element.72), channel_id=1, source_target_pairs={{0,30},{2,28},{4,26},{6,24},{8,22},{10,20},{12,18},{14,16},{16,14}... | collective-permute-start | bytes 688136 | tf_op jit(solution)/shard_map/ppermute | solution.py:289
  190.4 9.2 %collective-permute-start.27 = (bf16[128,1024]{1,0:T(8,128)(2,1)S(1)}, bf16[128,1024]{1,0:T(8,128)(2,1)S(1)}, u32[]{:S(2)}, u32[]{:S(2)}) collective-permute-start(bf16[128,1024]{1,0:T(8,128)(2,1)S(1)} %slice.101), channel_id=1, source_target_pairs={{0,1},{1,0},{2,3},{3,2},{4,5},{5,4},{6,7},{7,6},{8,9},{9,8},{10,11... | collective-permute-start | bytes 786440 | tf_op jit(solution)/shard_map/ppermute | solution.py:289
  191.0 14.3 %collective-permute-start.24 = (bf16[128,1024]{1,0:T(8,128)(2,1)S(1)}, bf16[128,1024]{1,0:T(8,128)(2,1)S(1)}, u32[]{:S(2)}, u32[]{:S(2)}) collective-permute-start(bf16[128,1024]{1,0:T(8,128)(2,1)S(1)} %multiply_convert_fusion.1), channel_id=1, source_target_pairs={{0,1},{1,0},{2,3},{3,2},{4,5},{5,4},{6,7},{7,6},{8,9},{9,8},{10,11... | collective-permute-start | bytes 786440 | tf_op jit(solution)/shard_map/ppermute | solution.py:289
  199.8 23.3 %collective-permute-start.28 = (bf16[128,1024]{1,0:T(8,128)(2,1)S(1)}, bf16[128,1024]{1,0:T(8,128)(2,1)S(1)}, u32[]{:S(2)}, u32[]{:S(2)}) collective-permute-start(bf16[128,1024]{1,0:T(8,128)(2,1)S(1)} %multiply_convert_fusion), channel_id=1, source_target_pairs={{0,1},{1,0},{2,3},{3,2},{4,5},{5,4},{6,7},{7,6},{8,9},{9,8},{10,11... | collective-permute-start | bytes 786440 | tf_op jit(solution)/shard_map/ppermute | solution.py:289
  205.3 39.6 %collective-permute-start.25 = (bf16[256,1024]{1,0:T(8,128)(2,1)S(1)}, bf16[256,1024]{1,0:T(8,128)(2,1)S(1)}, u32[]{:S(2)}, u32[]{:S(2)}) collective-permute-start(bf16[256,1024]{1,0:T(8,128)(2,1)S(1)} %constant_dynamic-update-slice_fusion.refs_1_), channel_id=1, source_target_pairs={{0,16},{2,18},{4,20},{6,22},{8,24},{10,26},{12,28},{14,30},{16,0},... | collective-permute-start | bytes 1572872 | tf_op jit(solution)/shard_map/ppermute | solution.py:289
  223.2 21.7 %collective-permute-start.29 = (bf16[256,1024]{1,0:T(8,128)(2,1)S(1)}, bf16[256,1024]{1,0:T(8,128)(2,1)S(1)}, u32[]{:S(2)}, u32[]{:S(2)}) collective-permute-start(bf16[256,1024]{1,0:T(8,128)(2,1)S(1)} %pad_maximum_fusion.2.refs_5_), channel_id=1, source_target_pairs={{0,2},{2,0},{4,6},{6,4},{8,10},{10,8},{12,14},{14,12},{16,18},{18,... | collective-permute-start | bytes 1572872 | tf_op jit(solution)/shard_map/ppermute | solution.py:289
  256.1 6.7 %collective-permute-start.30 = (bf16[128,1792]{1,0:T(8,128)(2,1)}, bf16[128,1792]{1,0:T(8,128)(2,1)S(1)}, u32[]{:S(2)}, u32[]{:S(2)}) collective-permute-start(bf16[128,1792]{1,0:T(8,128)(2,1)} %get-tuple-element.98), channel_id=1, source_target_pairs={{0,2},{2,0},{4,6},{6,4},{8,10},{10,8},{12,14},{14,12},{16,18},{18,... | collective-permute-start | bytes 1376264 | tf_op jit(solution)/shard_map/ppermute | solution.py:289
  260.7 8.6 %collective-permute-start.38 = (bf16[2,16,1792]{2,1,0:T(8,128)(2,1)S(1)}, bf16[2,16,1792]{2,1,0:T(8,128)(2,1)S(1)}, u32[]{:S(2)}, u32[]{:S(2)}) collective-permute-start(bf16[2,16,1792]{2,1,0:T(8,128)(2,1)S(1)} %get-tuple-element.114), channel_id=1, source_target_pairs={{0,12},{2,14},{4,8},{6,10},{8,4},{10,6},{12,0},{14,2},{16,28},{18,... | collective-permute-start | bytes 344072 | tf_op jit(solution)/shard_map/ppermute | solution.py:289
  263.0 8.0 %collective-permute-start.31 = (bf16[2,16,1792]{2,1,0:T(8,128)(2,1)S(1)}, bf16[2,16,1792]{2,1,0:T(8,128)(2,1)S(1)}, u32[]{:S(2)}, u32[]{:S(2)}) collective-permute-start(bf16[2,16,1792]{2,1,0:T(8,128)(2,1)S(1)} %get-tuple-element.115), channel_id=1, source_target_pairs={{0,4},{2,6},{4,0},{6,2},{8,12},{10,14},{12,8},{14,10},{16,20},{18,... | collective-permute-start | bytes 344072 | tf_op jit(solution)/shard_map/ppermute | solution.py:289
  264.4 7.8 %collective-permute-start.32 = (bf16[2,16,1792]{2,1,0:T(8,128)(2,1)S(1)}, bf16[2,16,1792]{2,1,0:T(8,128)(2,1)S(1)}, u32[]{:S(2)}, u32[]{:S(2)}) collective-permute-start(bf16[2,16,1792]{2,1,0:T(8,128)(2,1)S(1)} %get-tuple-element.116), channel_id=1, source_target_pairs={{0,8},{2,10},{4,12},{6,14},{8,0},{10,2},{12,4},{14,6},{16,24},{18,... | collective-permute-start | bytes 344072 | tf_op jit(solution)/shard_map/ppermute | solution.py:289
  264.6 9.2 %collective-permute-start.33 = (bf16[2,16,1792]{2,1,0:T(8,128)(2,1)S(1)}, bf16[2,16,1792]{2,1,0:T(8,128)(2,1)S(1)}, u32[]{:S(2)}, u32[]{:S(2)}) collective-permute-start(bf16[2,16,1792]{2,1,0:T(8,128)(2,1)S(1)} %get-tuple-element.117), channel_id=1, source_target_pairs={{0,12},{2,14},{4,8},{6,10},{8,4},{10,6},{12,0},{14,2},{16,28},{18,... | collective-permute-start | bytes 344072 | tf_op jit(solution)/shard_map/ppermute | solution.py:289
  269.4 6.5 %collective-permute-start.39 = (bf16[16,1792]{1,0:T(8,128)(2,1)S(1)}, bf16[16,1792]{1,0:T(8,128)(2,1)S(1)}, u32[]{:S(2)}, u32[]{:S(2)}) collective-permute-start(bf16[16,1792]{1,0:T(8,128)(2,1)S(1)} %slice_bitcast_fusion.8), channel_id=1, source_target_pairs={{0,16},{2,18},{4,20},{6,22},{8,24},{10,26},{12,28},{14,30},{16,0},... | collective-permute-start | bytes 172040 | tf_op jit(solution)/shard_map/ppermute | solution.py:289
  (39 other events, 429.7 us)
